TPU v7x, 32 devices: a whole 2x2x4 slice. The times are simulated.
32 devices in a mesh: grp: 2 (over x), row: 4 (over y, core), diag: 4 (over z).
Axes of the slice: x: 2, y: 2, z: 4, core: 2. Of those that a mesh axis runs over, the one named last changes fastest.
Arguments:
- emb_rows: bfloat16 [32, 1024], P(None, ('grp', 'row')), parts along dimension 1, may hold values from -6 to 6
- emb_cols: bfloat16 [32, 1024], P(None, ('grp', 'row')), parts along dimension 1, may hold values from -6 to 6
- kernel: bfloat16 [3, 3, 32, 32], replicated, may hold values from -0.375 to 0.375
- bias: float32 [32], replicated, may hold values from -3 to 3
- cotangent: bfloat16 [32, 1024, 512], P(None, ('grp', 'row'), 'diag'), parts along dimension 1, may hold values from -6 to 6
- valid: int32 [1024], P(('grp', 'row')), parts along dimension 0, may hold values 0 or 1
- dilation: int32 [2], P('grp'), parts along dimension 0, may hold values from 1 to 4
- band: int32 [2], P('grp'), parts along dimension 0, may hold values from 384 to 512
Outputs:
- pair_out: bfloat16 [32, 1024, 512], P(None, ('grp', 'row'), 'diag'), parts along dimension 1
- row_grad: float32 [32, 1024], P(None, ('grp', 'row')), parts along dimension 1
- col_grad: float32 [32, 1024], P(None, ('grp', 'row')), parts along dimension 1
- kernel_grad: float32 [6, 3, 32, 32], P('grp'), parts along dimension 0
- bias_grad: float32 [64], P('grp'), parts along dimension 0
There are 2 independent parts, one for each index of `grp`. A program takes and returns all parts, laid end to end along the dimension named above; an argument that names none is the same for every part. Nothing has to cross between parts.
All inputs are finite; a program needn't handle non-finite values. No bound on the sum of `valid` on one device may be relied on, other than what follows from the above.
Results may differ from a plain program's by a relative error of at most 0.0032.
Values may be sent and summed in bfloat16 or wider, within the bound.
No kernel may reach another device: no remote copies, remote signals or barrier semaphores. Data moves between devices by JAX's collectives and lax.ppermute only.
A program may use at most 128 MiB of HBM per device.

v0:
```python
import jax
import jax.numpy as jnp
from jax import lax
from jax.sharding import PartitionSpec as P

MAXDIL = 4


def passed_along(value, axis, steps):
    count = lax.axis_size(axis)
    initial, last = (max(0, -steps), min(count, count - steps))
    return lax.ppermute(value, axis, [(source, source + steps) for source in range(initial, last)])


def with_halo(array, sides, width):
    for axis, dim in sides:
        size, length = (lax.axis_size(axis), array.shape[dim])
        up = [(i, (i + 1) % size) for i in range(size - 1)]
        down = [(j, i) for i, j in up]
        last = lax.slice_in_dim(array, length - width, length, axis=dim)
        initial = lax.slice_in_dim(array, 0, width, axis=dim)
        before = lax.ppermute(last, axis, up)
        after = lax.ppermute(initial, axis, down)
        array = jnp.concatenate([before, array, after], axis=dim)
    return array


def diagonal_take(window, row_number, diagonal_number):
    span_width = row_number + diagonal_number - 1
    leading = window.shape[:-1]
    widened = jnp.broadcast_to(window[..., None, :], leading + (row_number, span_width))
    flattened = widened.reshape(leading + (row_number * span_width,))
    flattened = jnp.pad(flattened, [(0, 0)] * len(leading) + [(0, row_number)])
    return flattened.reshape(leading + (row_number, span_width + 1))[..., :diagonal_number]


def diagonal_fold(field):
    channels, row_number, diagonal_number = field.shape
    span_width = row_number + diagonal_number - 1
    padded = jnp.pad(field, ((0, 0), (0, 0), (0, span_width + 1 - diagonal_number)))
    flattened = padded.reshape(channels, row_number * (span_width + 1))[
        :, : row_number * span_width
    ]
    return jnp.sum(flattened.reshape(channels, row_number, span_width), axis=1)


def diagonal_sums(field):
    channels, row_number, diagonal_number = field.shape
    block_row_list = 128

    def accumulate(index, totals):
        return totals + diagonal_fold(field)

    totals = jnp.zeros((channels, row_number + diagonal_number - 1), jnp.float32)
    return lax.fori_loop(0, row_number // block_row_list, accumulate, totals)


def pair_block(
    row_embed, row_valid, col_window, col_valid, first_diag, row_number, diagonal_number, band_limit
):
    outer = row_embed.astype(jnp.float32)[:, :, None] + diagonal_take(
        col_window, row_number, diagonal_number
    ).astype(jnp.float32)
    offsets = first_diag + jnp.arange(diagonal_number, dtype=jnp.int32)
    inside = ((offsets >= 0) & (offsets < band_limit)).astype(jnp.float32)
    validity = (
        row_valid[:, None]
        * diagonal_take(col_valid[None], row_number, diagonal_number)[0]
        * inside[None, :]
    )
    hidden = outer * validity
    active = (jax.nn.gelu(hidden) * validity).astype(jnp.bfloat16)
    return (hidden, validity, active)


def contract(form, left, right):
    return jnp.einsum(form, left, right, preferred_element_type=jnp.float32)


def dilated_convolve(
    active_extended, kernel, dilation_factor, row_number, diagonal_number, border_width
):
    channels = active_extended.shape[0]
    result = jnp.zeros((kernel.shape[2], row_number, diagonal_number), jnp.float32)
    for kernel_tap_row in range(3):
        for kernel_tap_column in range(3):
            corner_patch = (
                jnp.int32(0),
                border_width + (kernel_tap_row - 1) * dilation_factor,
                border_width + (kernel_tap_column - kernel_tap_row) * dilation_factor,
            )
            piece = lax.dynamic_slice(
                active_extended, corner_patch, (channels, row_number, diagonal_number)
            )
            result = result + contract(
                "oc,crk->ork", kernel[kernel_tap_row, kernel_tap_column], piece
            )
    return result


def kernel_summands(
    gradient_local, active_extended, dilation_factor, row_number, diagonal_number, border_width
):
    channels = active_extended.shape[0]
    taps = []
    for kernel_tap_row in range(3):
        for kernel_tap_column in range(3):
            corner_patch = (
                jnp.int32(0),
                border_width + (kernel_tap_row - 1) * dilation_factor,
                border_width + (kernel_tap_column - kernel_tap_row) * dilation_factor,
            )
            piece = lax.dynamic_slice(
                active_extended, corner_patch, (channels, row_number, diagonal_number)
            )
            taps.append(contract("ork,crk->oc", gradient_local, piece))
    return jnp.stack(taps).reshape(3, 3, channels, channels)


def dilated_convolve_grad(
    gradient_extended, kernel, dilation_factor, row_number, diagonal_number, border_width
):
    channels = gradient_extended.shape[0]
    result = jnp.zeros((kernel.shape[3], row_number, diagonal_number), jnp.float32)
    for kernel_tap_row in range(3):
        for kernel_tap_column in range(3):
            corner_patch = (
                jnp.int32(0),
                border_width - (kernel_tap_row - 1) * dilation_factor,
                border_width - (kernel_tap_column - kernel_tap_row) * dilation_factor,
            )
            piece = lax.dynamic_slice(
                gradient_extended, corner_patch, (channels, row_number, diagonal_number)
            )
            result = result + contract(
                "oc,ork->crk", kernel[kernel_tap_row, kernel_tap_column], piece
            )
    return result


def local(emb_rows, emb_cols, kernel, bias, cotangent, valid, dilation, band):
    channels, row_number = emb_rows.shape
    diagonal_number = cotangent.shape[2]
    border_width = 2 * MAXDIL
    row_devices = lax.axis_size("row")
    total_diags = diagonal_number * lax.axis_size("diag")
    reach = (total_diags + 2 * border_width + row_number - 1) // row_number
    first_diag = lax.axis_index("diag") * diagonal_number
    dilation_factor = dilation[0]
    band_limit = band[0]
    valid_half = valid.astype(jnp.bfloat16)
    col_pieces = [emb_cols]
    valid_pieces = [valid_half]
    for offset in range(1, reach + 1):
        moved_cols, moved_valid = passed_along((emb_cols, valid_half), "row", -offset)
        col_pieces.append(moved_cols)
        valid_pieces.append(moved_valid)
    before_cols, before_valid = passed_along((emb_cols, valid_half), "row", 1)
    ext_cols = jnp.concatenate([before_cols] + col_pieces, axis=1)
    ext_valid = jnp.concatenate([before_valid] + valid_pieces, axis=0).astype(jnp.float32)
    row_embed = with_halo(emb_rows, (("row", 1),), border_width)
    span = row_number + diagonal_number + 4 * border_width - 1
    window_start = row_number + first_diag - 2 * border_width
    col_window = lax.dynamic_slice_in_dim(ext_cols, window_start, span, 1)
    col_valid = lax.dynamic_slice_in_dim(ext_valid, window_start, span, 0)
    row_valid = ext_valid[row_number - border_width : 2 * row_number + border_width]
    hidden_ext, valid_ext, active_extended = pair_block(
        row_embed,
        row_valid,
        col_window,
        col_valid,
        first_diag - border_width,
        row_number + 2 * border_width,
        diagonal_number + 2 * border_width,
        band_limit,
    )
    hidden = hidden_ext[
        :, border_width : border_width + row_number, border_width : border_width + diagonal_number
    ]
    validity = valid_ext[
        border_width : border_width + row_number, border_width : border_width + diagonal_number
    ]
    mixed_features = (
        dilated_convolve(
            active_extended, kernel, dilation_factor, row_number, diagonal_number, border_width
        )
        + bias[:, None, None]
    )
    pair_out = ((hidden + mixed_features) * validity).astype(jnp.bfloat16)
    gradient_local = (cotangent.astype(jnp.float32) * validity).astype(jnp.bfloat16)
    gradient_extended = with_halo(gradient_local, (("row", 1), ("diag", 2)), border_width)
    kernel_portion = kernel_summands(
        gradient_local, active_extended, dilation_factor, row_number, diagonal_number, border_width
    )
    bias_part = jnp.sum(gradient_local.astype(jnp.float32), axis=(1, 2))
    activation_grad = dilated_convolve_grad(
        gradient_extended, kernel, dilation_factor, row_number, diagonal_number, border_width
    )
    unused, pullback = jax.vjp(jax.nn.gelu, hidden)
    dpair = (
        gradient_local.astype(jnp.float32) + pullback(activation_grad * validity)[0]
    ) * validity
    row_part = jnp.sum(dpair, axis=2)
    col_part = diagonal_sums(dpair)
    spread = jnp.zeros((channels, (reach + 1) * row_number), jnp.float32)
    spread = lax.dynamic_update_slice_in_dim(spread, col_part, first_diag, 1)
    col_sum = spread[:, :row_number]
    for offset in range(1, reach + 1):
        piece = spread[:, offset * row_number : (offset + 1) * row_number]
        col_sum = col_sum + passed_along(piece, "row", offset)
    row_sum, col_total = lax.psum((row_part, col_sum), "diag")
    kernel_total, bias_total = lax.psum((kernel_portion, bias_part), ("row", "diag"))
    embed_scale = 1.0 / jnp.sqrt(jnp.float32(total_diags))
    weight_scale = 1.0 / jnp.sqrt(jnp.float32(row_devices * row_number) * jnp.float32(total_diags))
    return (
        pair_out,
        row_sum * embed_scale,
        col_total * embed_scale,
        kernel_total * weight_scale,
        bias_total * weight_scale,
    )


def solution(mesh):
    in_specs = (
        P(None, ("grp", "row")),
        P(None, ("grp", "row")),
        P(),
        P(),
        P(None, ("grp", "row"), "diag"),
        P(("grp", "row")),
        P("grp"),
        P("grp"),
    )
    out_specs = (
        P(None, ("grp", "row"), "diag"),
        P(None, ("grp", "row")),
        P(None, ("grp", "row")),
        P("grp", None, None, None),
        P("grp"),
    )
    return jax.shard_map(local, mesh=mesh, in_specs=in_specs, out_specs=out_specs, check_vma=False)
```

profile of v0, /device:TPU:0, one launch (start us, length us, event | category | flops | bytes accessed | tf_op | source)
XLA Modules:
  0.0 238.5 jit_solution(15318157826877124595)
XLA Ops:
  0.6 0.7 convert_element_type.48
  1.4 2.4 collective-permute-start.7
  3.8 1.3 collective-permute-start.8
  5.1 1.3 collective-permute-start.9
  6.4 1.3 collective-permute-start.10
  7.7 0.7 collective-permute-start.11
  9.7 0.8 fusion.152
  10.6 0.8 collective-permute-start.6
  11.8 5.1 %collective-permute-start.2 = (bf16[32,128]{1,0:T(8,128)(2,1)}, bf16[32,128]{1,0:T(8,128)(2,1)}, u32[]{:S(2)}, u32[]{:S(2)}) collective-permute-start(bf16[32,128]{1,0:T(8,128)(2,1)} %param.9), channel_id=1, source_target_pairs={{0,4},{4,8},{8,12},{1,5},{5,9},{9,13},{2,6},{6,10},{10,14},{3,7},{... | collective-permute-start | bytes 24584 | tf_op jit(solution)/shard_map/ppermute | solution.py:12
  17.1 1.3 collective-permute-start.3
  18.6 3.7 %collective-permute-start = (bf16[32,8]{1,0:T(8,128)(2,1)S(1)}, bf16[32,8]{1,0:T(8,128)(2,1)S(1)}, u32[]{:S(2)}, u32[]{:S(2)}) collective-permute-start(bf16[32,8]{1,0:T(8,128)(2,1)S(1)} %get-tuple-element.53), channel_id=1, source_target_pairs={{0,4},{4,8},{8,12},{1,5},{5,9},{9,13},{2,6},{6,10},{10,14},{3,7},{... | collective-permute-start | bytes 1544 | tf_op jit(solution)/shard_map/ppermute | solution.py:22
  22.6 1.3 collective-permute-start.1
  25.8 1.4 convert_reduce_fusion
  27.7 0.7 fusion.150
  28.3 1.3 collective-permute-start.4
  29.6 1.3 collective-permute-start.5
  31.1 4.9 %collective-permute-start.12 = (bf16[32,8,128]{2,0,1:T(8,128)(2,1)}, bf16[32,8,128]{2,0,1:T(8,128)(2,1)}, u32[]{:S(2)}, u32[]{:S(2)}) collective-permute-start(bf16[32,8,128]{2,0,1:T(8,128)(2,1)} %get-tuple-element.44), channel_id=1, source_target_pairs={{0,4},{4,8},{8,12},{1,5},{5,9},{9,13},{2,6},{6,10},{10,14},{3,7},{... | collective-permute-start | bytes 196616 | tf_op jit(solution)/shard_map/ppermute | solution.py:22
  36.0 0.7 constant_dynamic-update-slice_fusion.6
  36.7 1.3 collective-permute-start.13
  38.0 0.7 constant_dynamic-update-slice_fusion.4
  38.7 0.7 constant_dynamic-update-slice_fusion.3
  39.4 0.7 constant_dynamic-update-slice_fusion.2
  40.2 2.1 broadcast_in_dim.8
  42.3 6.1 %reshape.120 = bf16[32,41328]{1,0:T(8,128)(2,1)} reshape(bf16[32,144,287]{2,1,0:T(8,128)(2,1)} %broadcast_in_dim.8) | data formatting | bytes 5289984 | tf_op jit(solution)/shard_map/reshape | solution.py:32
  48.3 3.4 %pad.13 = bf16[32,41472]{1,0:T(8,128)(2,1)} pad(bf16[32,41328]{1,0:T(8,128)(2,1)} %reshape.120, bf16[]{:T(256)} %constant.75.clone.1), padding=0_0x0_144 | pad | bytes 5299202 | tf_op jit(solution)/shard_map/jit(_pad)/pad | solution.py:33
  51.7 7.4 %reshape.121 = bf16[32,144,288]{2,1,0:T(8,128)(2,1)} reshape(bf16[32,41472]{1,0:T(8,128)(2,1)} %pad.13) | data formatting | bytes 5308416 | tf_op jit(solution)/shard_map/reshape | solution.py:34
  59.2 1.7 slice-done
  60.9 2.2 add_multiply_fusion
  63.6 0.6 fusion.69
  64.2 0.6 fusion.60
  67.5 0.6 fusion.66
  68.6 0.6 fusion.26
  69.1 0.6 fusion.25
  70.2 0.6 fusion.63
  71.4 0.6 fusion.22
  72.0 2.6 %fusion.20 = bf16[32,128,128]{2,0,1:T(8,128)(2,1)} fusion(f32[128,128,32]{1,2,0:T(8,128)S(1)} %fusion.60, f32[128,128,32]{1,2,0:T(8,128)S(1)} %fusion.63, f32[128,128,32]{1,2,0:T(8,128)S(1)} %fusion.51, f32[128,128,32]{1,2,0:T(8,128)S(1)} %fusion.46, f32[128,128,32]{1,2,0:T(8,128)S(1)} %fusion.54, f32[128,128,32]{1,2,0:T(8,128)S(1)} %fusion.66, ...), kind=kOutput, calls=%fused_computation.30 | convolution fusion | flops 39845888 | bytes 21045764 | tf_op jit(solution)/shard_map/oc,crk->ork/dot_general | solution.py:77
  75.2 80.3 %all-reduce.3 = (f32[3,3,32,32]{3,2,1,0:T(8,128)}, f32[32]{0:T(128)S(1)}) all-reduce(f32[3,3,32,32]{3,2,1,0:T(8,128)S(1)} %bitcast.175, f32[32]{0:T(128)S(1)} %copy-done.7), channel_id=1, replica_groups=mesh['grp'=2,'row'=4,'diag'=4] {'row','diag'}, use_global_device_ids=true, to_apply=%region_4.5 | all-reduce | flops 9248 | bytes 73984 | tf_op jit(solution)/shard_map/psum | solution.py:212
  155.6 1.0 pad_maximum_fusion.1
  156.6 2.0 fusion.149
  158.6 3.3 %copy.98 = bf16[32,144,8]{1,2,0:T(8,128)(2,1)} copy(bf16[32,144,8]{2,0,1:T(8,128)(2,1)} %get-tuple-element.42) | data formatting | bytes 147456 | tf_op jit(solution)/shard_map/slice | solution.py:20
  161.8 1.9 collective-permute-start.14
  163.8 3.2 %copy.99 = bf16[32,144,8]{1,2,0:T(8,128)(2,1)} copy(bf16[32,144,8]{2,0,1:T(8,128)(2,1)} %get-tuple-element.43) | data formatting | bytes 147456 | tf_op jit(solution)/shard_map/slice | solution.py:21
  167.0 1.3 collective-permute-start.15
  168.3 0.7 broadcast_multiply_fusion
  169.0 3.4 %copy.100 = bf16[32,144,8]{2,0,1:T(8,128)(2,1)} copy(bf16[32,144,8]{1,2,0:T(8,128)(2,1)} %collective-permute-done.14) | data formatting | bytes 147456 | tf_op jit(solution)/shard_map/ppermute | solution.py:22
  172.4 1.7 collective-permute-done.15
  174.2 3.4 %copy.101 = bf16[32,144,8]{2,0,1:T(8,128)(2,1)} copy(bf16[32,144,8]{1,2,0:T(8,128)(2,1)} %collective-permute-done.15) | data formatting | bytes 147456 | tf_op jit(solution)/shard_map/ppermute | solution.py:23
  177.6 3.4 %pad_maximum_fusion = bf16[32,144,144]{2,0,1:T(8,128)(2,1)S(1)} fusion(bf16[32,144,8]{2,0,1:T(8,128)(2,1)} %copy.101, bf16[32,8,128]{2,0,1:T(8,128)(2,1)} %collective-permute-done.13, bf16[32,128,128]{2,0,1:T(8,128)(2,1)S(1)} %get-tuple-element.39, bf16[32,8,128]{2,0,1:T(8,128)(2,1)} %collective-permute-done.12, bf16[32,144,8]{2,0,1:T(8,128)(2,1)} %copy.100), kind=kLoop, calls=%fused_computation.15 | loop fusion | flops 6635520 | bytes 2654208 | tf_op jit(solution)/shard_map/concatenate | solution.py:24
  184.7 4.7 %fusion.153 = (f32[32,128]{0,1:T(8,128)S(1)}, f32[32,128,128]{2,0,1:T(8,128)S(1)}) fusion(f32[128,128]{1,0:T(8,128)S(1)} %fusion.75, f32[32,144,144]{2,0,1:T(8,128)} %copy-done, bf16[3,3,32,32]{3,2,1,0:T(8,128)(2,1)S(1)} %copy-done.3, bf16[32,144,144]{2,0,1:T(8,128)(2,1)S(1)} %pad_maximum_fusion, s32[]{:T(128)S(6)} %select_n.26, ...), kind=kOutput, calls=%fused_computation.194 | convolution fusion | flops 50327552 | bytes 23224324 | tf_op jit(solution)/shard_map/oc,ork->crk/dot_general | solution.py:77
  189.3 1.2 copy.135
  191.1 2.4 %copy.136 = f32[4,8,128,256]{3,1,2,0:T(8,128)S(1)} copy(f32[4,8,128,256]{3,2,1,0:T(8,128)S(1)} %bitcast.173) | data formatting | bytes 8388608
  193.5 2.3 slice.128
  195.8 9.6 %reshape.124 = f32[32,128,255]{2,1,0:T(8,128)} reshape(f32[32,32640]{1,0:T(8,128)} %slice.128) | data formatting | bytes 8355840 | tf_op jit(solution)/shard_map/while/body/eval_jaxpr/reshape | solution.py:44
  205.3 2.7 %reduce_sum.29 = f32[32,255]{1,0:T(8,128)S(1)} reduce(f32[32,128,255]{2,1,0:T(8,128)} %reshape.124, f32[]{:T(128)} %constant.76.clone.1), dimensions={1}, to_apply=%region_2.3 | reduce | flops 1036320 | bytes 4210564 | tf_op jit(solution)/shard_map/while/body/eval_jaxpr/reduce_sum | solution.py:44
  208.2 1.0 dynamic_update_slice.3
  209.2 1.3 collective-permute-start.16
  210.5 2.9 %collective-permute-start.17 = (f32[32,128]{0,1:T(8,128)S(1)}, f32[32,128]{0,1:T(8,128)S(1)}, u32[]{:S(2)}, u32[]{:S(2)}) collective-permute-start(f32[32,128]{0,1:T(8,128)S(1)} %get-tuple-element.50), channel_id=1, source_target_pairs={{0,8},{4,12},{1,9},{5,13},{2,10},{6,14},{3,11},{7,15},{16,24},{20,... | collective-permute-start | bytes 49160 | tf_op jit(solution)/shard_map/ppermute | solution.py:12
  213.4 1.3 collective-permute-start.18
  214.7 0.7 collective-permute-start.19
  215.4 0.7 collective-permute-start.20
  216.5 1.4 copy.113
  218.0 18.9 %all-reduce.4 = (f32[32,128]{0,1:T(8,128)S(1)}, f32[32,128]{0,1:T(8,128)S(1)}) all-reduce(f32[32,128]{0,1:T(8,128)S(1)} %get-tuple-element.55, f32[32,128]{0,1:T(8,128)S(1)} %fusion.74), channel_id=1, replica_groups=mesh['grp'=2,'row'=4,'diag'=4] {'diag'}, use_global_device_ids=true, to_apply=%region_1.2 | all-reduce | flops 8192 | bytes 65536 | tf_op jit(solution)/shard_map/psum | solution.py:211
  236.9 0.7 copy.114
  237.6 0.7 copy.115
  (89 shorter events, 14.1 us)
Async XLA Ops:
  0.6 25.1 %copy-start.2 = (bf16[32,128,128]{2,1,0:T(8,128)(2,1)S(1)}, bf16[32,128,128]{2,1,0:T(8,128)(2,1)}, u32[]{:S(2)}) copy-start(bf16[32,128,128]{2,1,0:T(8,128)(2,1)} %param.12) | copy-start | bytes 3145732
  1.4 9.2 %collective-permute-start.7 = (bf16[128]{0:T(256)(128)(2,1)S(1)}, bf16[128]{0:T(256)(128)(2,1)S(1)}, u32[]{:S(2)}, u32[]{:S(2)}) collective-permute-start(bf16[128]{0:T(256)(128)(2,1)S(1)} %convert_element_type.48), channel_id=1, source_target_pairs={{0,4},{4,8},{8,12},{1,5},{5,9},{9,13},{2,6},{6,10},{10,14},{3,7},{... | collective-permute-start | bytes 776 | tf_op jit(solution)/shard_map/ppermute | solution.py:12
  3.8 8.0 %collective-permute-start.8 = (bf16[128]{0:T(256)(128)(2,1)S(1)}, bf16[128]{0:T(256)(128)(2,1)S(1)}, u32[]{:S(2)}, u32[]{:S(2)}) collective-permute-start(bf16[128]{0:T(256)(128)(2,1)S(1)} %convert_element_type.48), channel_id=1, source_target_pairs={{4,0},{8,4},{12,8},{5,1},{9,5},{13,9},{6,2},{10,6},{14,10},{7,3},{... | collective-permute-start | bytes 776 | tf_op jit(solution)/shard_map/ppermute | solution.py:12
  5.1 12.0 %collective-permute-start.9 = (bf16[128]{0:T(256)(128)(2,1)S(1)}, bf16[128]{0:T(256)(128)(2,1)S(1)}, u32[]{:S(2)}, u32[]{:S(2)}) collective-permute-start(bf16[128]{0:T(256)(128)(2,1)S(1)} %convert_element_type.48), channel_id=1, source_target_pairs={{8,0},{12,4},{9,1},{13,5},{10,2},{14,6},{11,3},{15,7},{24,16},{28,... | collective-permute-start | bytes 776 | tf_op jit(solution)/shard_map/ppermute | solution.py:12
  6.4 12.3 %collective-permute-start.10 = (bf16[128]{0:T(256)(128)(2,1)S(1)}, bf16[128]{0:T(256)(128)(2,1)S(1)}, u32[]{:S(2)}, u32[]{:S(2)}) collective-permute-start(bf16[128]{0:T(256)(128)(2,1)S(1)} %convert_element_type.48), channel_id=1, source_target_pairs={{12,0},{13,1},{14,2},{15,3},{28,16},{29,17},{30,18},{31,19}} | collective-permute-start | bytes 776 | tf_op jit(solution)/shard_map/ppermute | solution.py:12
  7.7 14.9 %collective-permute-start.11 = (bf16[128]{0:T(256)(128)(2,1)S(1)}, bf16[128]{0:T(256)(128)(2,1)S(1)}, u32[]{:S(2)}, u32[]{:S(2)}) collective-permute-start(bf16[128]{0:T(256)(128)(2,1)S(1)} %convert_element_type.48), channel_id=1, source_target_pairs={} | collective-permute-start | bytes 776 | tf_op jit(solution)/shard_map/ppermute | solution.py:12
  10.6 16.6 %copy-start.3 = (bf16[3,3,32,32]{3,2,1,0:T(8,128)(2,1)S(1)}, bf16[3,3,32,32]{3,2,1,0:T(8,128)(2,1)}, u32[]{:S(2)}) copy-start(bf16[3,3,32,32]{3,2,1,0:T(8,128)(2,1)} %param.10) | copy-start | bytes 55300
  10.6 29.5 %collective-permute-start.6 = (bf16[32,128]{1,0:T(8,128)(2,1)}, bf16[32,128]{1,0:T(8,128)(2,1)S(1)}, u32[]{:S(2)}, u32[]{:S(2)}) collective-permute-start(bf16[32,128]{1,0:T(8,128)(2,1)} %param.9), channel_id=1, source_target_pairs={} | collective-permute-start | bytes 24584 | tf_op jit(solution)/shard_map/ppermute | solution.py:12
  11.8 19.3 %collective-permute-start.2 = (bf16[32,128]{1,0:T(8,128)(2,1)}, bf16[32,128]{1,0:T(8,128)(2,1)}, u32[]{:S(2)}, u32[]{:S(2)}) collective-permute-start(bf16[32,128]{1,0:T(8,128)(2,1)} %param.9), channel_id=1, source_target_pairs={{0,4},{4,8},{8,12},{1,5},{5,9},{9,13},{2,6},{6,10},{10,14},{3,7},{... | collective-permute-start | bytes 24584 | tf_op jit(solution)/shard_map/ppermute | solution.py:12
  17.1 19.6 %collective-permute-start.3 = (bf16[32,128]{1,0:T(8,128)(2,1)}, bf16[32,128]{1,0:T(8,128)(2,1)}, u32[]{:S(2)}, u32[]{:S(2)}) collective-permute-start(bf16[32,128]{1,0:T(8,128)(2,1)} %param.9), channel_id=1, source_target_pairs={{4,0},{8,4},{12,8},{5,1},{9,5},{13,9},{6,2},{10,6},{14,10},{7,3},{... | collective-permute-start | bytes 24584 | tf_op jit(solution)/shard_map/ppermute | solution.py:12
  18.6 9.7 %collective-permute-start = (bf16[32,8]{1,0:T(8,128)(2,1)S(1)}, bf16[32,8]{1,0:T(8,128)(2,1)S(1)}, u32[]{:S(2)}, u32[]{:S(2)}) collective-permute-start(bf16[32,8]{1,0:T(8,128)(2,1)S(1)} %get-tuple-element.53), channel_id=1, source_target_pairs={{0,4},{4,8},{8,12},{1,5},{5,9},{9,13},{2,6},{6,10},{10,14},{3,7},{... | collective-permute-start | bytes 1544 | tf_op jit(solution)/shard_map/ppermute | solution.py:22
  22.6 7.0 %collective-permute-start.1 = (bf16[32,8]{1,0:T(8,128)(2,1)S(1)}, bf16[32,8]{1,0:T(8,128)(2,1)S(1)}, u32[]{:S(2)}, u32[]{:S(2)}) collective-permute-start(bf16[32,8]{1,0:T(8,128)(2,1)S(1)} %get-tuple-element.54), channel_id=1, source_target_pairs={{4,0},{8,4},{12,8},{5,1},{9,5},{13,9},{6,2},{10,6},{14,10},{7,3},{... | collective-permute-start | bytes 1544 | tf_op jit(solution)/shard_map/ppermute | solution.py:23
  27.2 1.1 copy-start.6
  27.2 3.7 %copy-start.5 = (bf16[32,128]{1,0:T(8,128)(2,1)S(1)}, bf16[32,128]{1,0:T(8,128)(2,1)}, u32[]{:S(2)}) copy-start(bf16[32,128]{1,0:T(8,128)(2,1)} %param.8) | copy-start | bytes 24580
  28.3 10.4 %collective-permute-start.4 = (bf16[32,128]{1,0:T(8,128)(2,1)S(1)}, bf16[32,128]{1,0:T(8,128)(2,1)}, u32[]{:S(2)}, u32[]{:S(2)}) collective-permute-start(bf16[32,128]{1,0:T(8,128)(2,1)S(1)} %copy-done.6), channel_id=1, source_target_pairs={{8,0},{12,4},{9,1},{13,5},{10,2},{14,6},{11,3},{15,7},{24,16},{28,... | collective-permute-start | bytes 24584 | tf_op jit(solution)/shard_map/ppermute | solution.py:12
  29.6 9.8 %collective-permute-start.5 = (bf16[32,128]{1,0:T(8,128)(2,1)S(1)}, bf16[32,128]{1,0:T(8,128)(2,1)}, u32[]{:S(2)}, u32[]{:S(2)}) collective-permute-start(bf16[32,128]{1,0:T(8,128)(2,1)S(1)} %copy-done.6), channel_id=1, source_target_pairs={{12,0},{13,1},{14,2},{15,3},{28,16},{29,17},{30,18},{31,19}} | collective-permute-start | bytes 24584 | tf_op jit(solution)/shard_map/ppermute | solution.py:12
  31.1 124.4 %collective-permute-start.12 = (bf16[32,8,128]{2,0,1:T(8,128)(2,1)}, bf16[32,8,128]{2,0,1:T(8,128)(2,1)}, u32[]{:S(2)}, u32[]{:S(2)}) collective-permute-start(bf16[32,8,128]{2,0,1:T(8,128)(2,1)} %get-tuple-element.44), channel_id=1, source_target_pairs={{0,4},{4,8},{8,12},{1,5},{5,9},{9,13},{2,6},{6,10},{10,14},{3,7},{... | collective-permute-start | bytes 196616 | tf_op jit(solution)/shard_map/ppermute | solution.py:22
  36.7 118.9 %collective-permute-start.13 = (bf16[32,8,128]{2,0,1:T(8,128)(2,1)}, bf16[32,8,128]{2,0,1:T(8,128)(2,1)}, u32[]{:S(2)}, u32[]{:S(2)}) collective-permute-start(bf16[32,8,128]{2,0,1:T(8,128)(2,1)} %get-tuple-element.45), channel_id=1, source_target_pairs={{4,0},{8,4},{12,8},{5,1},{9,5},{13,9},{6,2},{10,6},{14,10},{7,3},{... | collective-permute-start | bytes 196616 | tf_op jit(solution)/shard_map/ppermute | solution.py:23
  59.2 1.7 slice-start
  63.1 8.8 %copy-start = (f32[32,144,144]{2,0,1:T(8,128)}, f32[32,144,144]{2,0,1:T(8,128)S(1)}, u32[]{:S(2)}) copy-start(f32[32,144,144]{2,0,1:T(8,128)S(1)} %get-tuple-element.40) | copy-start | bytes 7962628
  70.9 1.1 copy-start.8
  74.6 0.7 copy-start.7
  158.6 9.7 %copy-start.4 = (f32[3,3,32,32]{3,2,1,0:T(8,128)S(1)}, f32[3,3,32,32]{3,2,1,0:T(8,128)}, u32[]{:S(2)}) copy-start(f32[3,3,32,32]{3,2,1,0:T(8,128)} %get-tuple-element.34) | copy-start | bytes 110596
  161.8 7.2 %collective-permute-start.14 = (bf16[32,144,8]{1,2,0:T(8,128)(2,1)}, bf16[32,144,8]{1,2,0:T(8,128)(2,1)}, u32[]{:S(2)}, u32[]{:S(2)}) collective-permute-start(bf16[32,144,8]{1,2,0:T(8,128)(2,1)} %copy.98), channel_id=1, source_target_pairs={{0,1},{1,2},{2,3},{4,5},{5,6},{6,7},{8,9},{9,10},{10,11},{12,13},{... | collective-permute-start | bytes 221192 | tf_op jit(solution)/shard_map/ppermute | solution.py:22
  167.0 7.2 %collective-permute-start.15 = (bf16[32,144,8]{1,2,0:T(8,128)(2,1)}, bf16[32,144,8]{1,2,0:T(8,128)(2,1)}, u32[]{:S(2)}, u32[]{:S(2)}) collective-permute-start(bf16[32,144,8]{1,2,0:T(8,128)(2,1)} %copy.99), channel_id=1, source_target_pairs={{1,0},{2,1},{3,2},{5,4},{6,5},{7,6},{9,8},{10,9},{11,10},{13,12},{... | collective-permute-start | bytes 221192 | tf_op jit(solution)/shard_map/ppermute | solution.py:23
  205.3 11.2 %copy-start.1 = (bf16[32,128,128]{2,0,1:T(8,128)(2,1)S(1)}, bf16[32,128,128]{2,0,1:T(8,128)(2,1)}, u32[]{:S(2)}) copy-start(bf16[32,128,128]{2,0,1:T(8,128)(2,1)} %fusion.20) | copy-start | bytes 3145732
  209.2 8.7 %collective-permute-start.16 = (f32[32,128]{0,1:T(8,128)S(1)}, f32[32,128]{0,1:T(8,128)S(1)}, u32[]{:S(2)}, u32[]{:S(2)}) collective-permute-start(f32[32,128]{0,1:T(8,128)S(1)} %get-tuple-element.46), channel_id=1, source_target_pairs={{0,4},{4,8},{8,12},{1,5},{5,9},{9,13},{2,6},{6,10},{10,14},{3,7},{... | collective-permute-start | bytes 49160 | tf_op jit(solution)/shard_map/ppermute | solution.py:12
  210.5 7.4 %collective-permute-start.17 = (f32[32,128]{0,1:T(8,128)S(1)}, f32[32,128]{0,1:T(8,128)S(1)}, u32[]{:S(2)}, u32[]{:S(2)}) collective-permute-start(f32[32,128]{0,1:T(8,128)S(1)} %get-tuple-element.50), channel_id=1, source_target_pairs={{0,8},{4,12},{1,9},{5,13},{2,10},{6,14},{3,11},{7,15},{16,24},{20,... | collective-permute-start | bytes 49160 | tf_op jit(solution)/shard_map/ppermute | solution.py:12
  213.4 4.5 %collective-permute-start.18 = (f32[32,128]{0,1:T(8,128)S(1)}, f32[32,128]{0,1:T(8,128)S(1)}, u32[]{:S(2)}, u32[]{:S(2)}) collective-permute-start(f32[32,128]{0,1:T(8,128)S(1)} %get-tuple-element.49), channel_id=1, source_target_pairs={{0,12},{1,13},{2,14},{3,15},{16,28},{17,29},{18,30},{19,31}} | collective-permute-start | bytes 49160 | tf_op jit(solution)/shard_map/ppermute | solution.py:12
  214.7 3.2 %collective-permute-start.19 = (f32[32,128]{0,1:T(8,128)S(1)}, f32[32,128]{0,1:T(8,128)S(1)}, u32[]{:S(2)}, u32[]{:S(2)}) collective-permute-start(f32[32,128]{0,1:T(8,128)S(1)} %get-tuple-element.48), channel_id=1, source_target_pairs={} | collective-permute-start | bytes 49160 | tf_op jit(solution)/shard_map/ppermute | solution.py:12
  215.4 2.6 %collective-permute-start.20 = (f32[32,128]{0,1:T(8,128)S(1)}, f32[32,128]{0,1:T(8,128)S(1)}, u32[]{:S(2)}, u32[]{:S(2)}) collective-permute-start(f32[32,128]{0,1:T(8,128)S(1)} %get-tuple-element.47), channel_id=1, source_target_pairs={} | collective-permute-start | bytes 49160 | tf_op jit(solution)/shard_map/ppermute | solution.py:12
where the time goes:
time: 240 us; the launch traced here: 239 us
  blocking collectives  99.2 us (41%)
  local copies, waits for them, and re-layouts  63.4 us (26%)
  starting transfers between devices  37.8 us (16%)
  matrix products  20.6 us (9%)
  other arithmetic  12.9 us (5%)
  between operations  2.72 us (1%)
    psum x1, blocking collectives, local(): lax.psum((kernel_portion, bias_part), ('row', 'diag'))  80.3 us
    ppermute x15, starting transfers between devices, passed_along(): lax.ppermute(value, axis, [(source, source + steps) for source in range(i...  23.4 us
    dot_general x27, matrix products, contract(): return jnp.einsum(form, left, right, preferred_element_type=jnp.float32)  20.6 us
    psum x1, blocking collectives, local(): row_sum, col_total = lax.psum((row_part, col_sum), 'diag')  18.9 us
    unnamed x35, local copies, waits for them, and re-layouts  10.7 us
    ppermute x3, starting transfers between devices, with_halo(): before = lax.ppermute(last, axis, up)  10.5 us
    reshape x1, local copies, waits for them, and re-layouts, diagonal_fold(): return jnp.sum(flattened.reshape(channels, row_number, span_width), axis=1)  9.58 us
    reshape x2, local copies, waits for them, and re-layouts, diagonal_take(): flattened.reshape(leading + (row_number, span_width + 1))  7.58 us
  transfers between devices with their start and end apart: 21, of which 1 were waited for; matrix products, arithmetic and copies ran while one was open for 22% of the time, Pallas kernels for 0%

commit v1 on v0

v1 whole, which is shorter than its diff:
```python
import jax
import jax.numpy as jnp
from jax import lax
from jax.experimental import pallas as pl
from jax.experimental.pallas import tpu as pltpu
from jax.sharding import PartitionSpec as P

MAXDIL = 4
EDGE = 2 * MAXDIL
SLOT = 2 * EDGE
GELU_C = 0.7978845608028654
GELU_A = 0.044715


def gelu_and_slope(h):
    square = h * h
    t = jnp.tanh(h * (GELU_C + (GELU_C * GELU_A) * square))
    half = 0.5 * h
    one = 1.0 + t
    slope = 0.5 * one + half * (1.0 - t * t) * (GELU_C + (3.0 * GELU_C * GELU_A) * square)
    return half * one, slope


def tile_kernel(
    gathered, kernel, bias, cot, dil, band,
    pair_out, sums, kgrad,
    act_halo, taps, gtaps, hid, slope, vmask, gz, gedge, cols, colv, accs, kacc,
):
    ch = bias.shape[0]
    n = cot.shape[1]
    sub = ch // 8
    blocks = gathered.shape[0]
    extra = MAXDIL
    ext = n + 2 * extra
    packs = ext
    xhalo = ext + SLOT
    r_id = lax.axis_index("row")
    k_id = lax.axis_index("diag")
    r = dil[0]
    width = band[0] - k_id * n
    low = -k_id * n
    f32, bf16 = jnp.float32, jnp.bfloat16
    lane8 = lax.broadcasted_iota(jnp.int32, (8, n), 1)
    lane16 = lax.broadcasted_iota(jnp.int32, (16, n), 1)
    lim = {s: (s * r).astype(f32).astype(bf16) for s in (1, 2, -1, -2)}
    top = {s: (n - s * r).astype(f32).astype(bf16) for s in (1, 2)}

    def block_of(index, first, count):
        found = gathered[jnp.clip(index, 0, blocks - 1), first : first + count, :]
        inside = ((index >= 0) & (index < blocks)).astype(f32)
        return found.astype(f32) * inside

    for t in range(4):
        cols[t] = block_of(r_id + k_id + t - 1, 0, ch).reshape(sub, 8, n)
        colv[t] = block_of(r_id + k_id + t - 1, 2 * ch, 8)

    def row_values(index):
        return block_of(index, ch, ch), block_of(index, 2 * ch, 8)

    own, own_v = row_values(r_id)
    prev, prev_v = row_values(r_id - 1)
    nxt, nxt_v = row_values(r_id + 1)

    def unit(slot, rows, rows_v, col, col_v, inside):
        v = jnp.where(inside, rows_v * col_v, 0.0)
        h = (rows + col) * v[None]
        a, g = gelu_and_slope(h)
        slope[slot] = g * v[None]
        vmask[slot] = jnp.concatenate([v, v], axis=0).astype(bf16)
        return h, a.reshape(ch, n).astype(bf16)

    def spread(rows, at):
        return jnp.broadcast_to(rows[:, at : at + 1], rows.shape)

    def pick(t):
        col, col_v = cols[3], colv[3]
        for b in (2, 1, 0):
            here = t == b - 1
            col = jnp.where(here[None], cols[b], col)
            col_v = jnp.where(here, colv[b], col_v)
        return col, col_v

    for p in range(SLOT):
        loose = p + SLOT * ((lane8 - p + EDGE) >> 4)
        row = loose & (n - 1)
        e = lane8 - loose
        d = jnp.where(e < 0, e, e + n)
        col, col_v = pick((row + d) >> 7)
        index = jnp.concatenate([row] * sub, axis=0)
        rows = jnp.take_along_axis(own, index, axis=1).reshape(sub, 8, n)
        rows_v = jnp.take_along_axis(own_v, row, axis=1)
        _, a = unit(packs + p, rows, rows_v, col, col_v, (d >= low) & (d < width))
        act_halo[p] = a

    lane32 = lax.broadcasted_iota(jnp.int32, (ch, n), 1)
    near = jnp.where(lane32 < extra, pltpu.roll(prev, extra, 1), pltpu.roll(nxt, extra, 1))
    near_v = jnp.where(lane8 < extra, pltpu.roll(prev_v, extra, 1), pltpu.roll(nxt_v, extra, 1))
    near_rows = [y - extra if y < extra else n + y - extra for y in range(2 * extra)]
    for y, i in enumerate(near_rows):
        e = ((lane8 - i + EDGE) & (n - 1)) - EDGE
        d = jnp.where(e < 0, e, e + n)
        rows = spread(near, y).reshape(sub, 8, n)
        rows_v = spread(near_v, y)
        col, col_v = pick((i + d) >> 7)
        inside = (e < EDGE) & (d >= low) & (d < width)
        _, a = unit(xhalo + y, rows, rows_v, col, col_v, inside)
        act_halo[SLOT + y] = a

    def store_taps(i, a, halo):
        d = ((lane16 - i) & (n - 1)).astype(f32).astype(bf16)
        a2, h2 = a.reshape(2, 16, n), halo.reshape(2, 16, n)

        def sel(mask):
            return jnp.where(mask[None], h2, a2).reshape(ch, n)

        up1, up2 = sel(d < lim[1]), sel(d < lim[2])
        dn1, dn2 = sel(d >= top[1]), sel(d >= top[2])
        byshift = {0: a, 1: up1, 2: up2, -1: dn1, -2: dn2}
        back = n - r
        for ta in range(3):
            at = i - (ta - 1) * r + EDGE
            for tb in range(3):
                x = byshift[tb - ta]
                if tb == 0:
                    x = pltpu.roll(x, r, 1)
                elif tb == 2:
                    x = pltpu.roll(x, back, 1)
                tap = (3 * ta + tb) * ch
                taps[at, tap : tap + ch, :] = x

    for y, i in enumerate(near_rows):
        d = (lane8 - i) & (n - 1)
        rows = spread(near, y).reshape(sub, 8, n)
        rows_v = spread(near_v, y)
        col, col_v = pick((i + d) >> 7)
        _, a = unit(i + extra, rows, rows_v, col, col_v, (d >= low) & (d < width))
        store_taps(i, a, act_halo[SLOT + y])

    group = 8

    def rows_step(g, carry):
        base = g * group
        turned = pltpu.roll(own, (n - base) & (n - 1), 1)
        turned_v = pltpu.roll(own_v, (n - base) & (n - 1), 1)
        for u in range(group):
            i = base + u
            here = lane8 >= i
            col = jnp.where(here[None], cols[1], cols[2])
            col_v = jnp.where(here, colv[1], colv[2])
            d = (lane8 - i) & (n - 1)
            rows = spread(turned, u).reshape(sub, 8, n)
            h, a = unit(i + extra, rows, spread(turned_v, u), col, col_v, (d >= low) & (d < width))
            hid[i] = h
            store_taps(i, a, act_halo[i & (SLOT - 1)])
        return carry

    lax.fori_loop(0, n // group, rows_step, 0)

    for at in list(range(2 * extra)) + list(range(n, ext)) + list(range(xhalo, xhalo + 2 * extra)):
        gtaps[at] = jnp.zeros(gtaps.shape[1:], bf16)
    gedge[...] = jnp.zeros(gedge.shape, bf16)

    def turn(x, tb):
        if tb == 0:
            return pltpu.roll(x, n - r, 1)
        if tb == 2:
            return pltpu.roll(x, r, 1)
        return x

    def keep(x, mask):
        x2 = x.reshape(2, 16, n)
        return jnp.where(mask[None], x2, jnp.zeros_like(x2)).reshape(ch, n)

    def grads_step(g, carry):
        base = pl.multiple_of(g * 16, 16)
        block = jnp.swapaxes(cot[:, pl.ds(base, 16), :], 0, 1)
        for u in range(16):
            i = base + u
            x = pltpu.roll(block[u], i, 1)
            x = (x.reshape(2, 16, n) * vmask[i + extra][None]).reshape(ch, n)
            gz[i] = x
            d = ((lane16 - i) & (n - 1)).astype(f32).astype(bf16)
            slot = ((lane16 - i + EDGE) & (n - 1)).astype(f32).astype(bf16)
            old = gedge[u].reshape(2, 16, n)
            gedge[u] = jnp.where(
                (slot < jnp.array(SLOT, bf16))[None], x.reshape(2, 16, n), old
            ).reshape(ch, n)
            byshift = {0: x}
            for s in (1, 2):
                byshift[s] = keep(x, d < top[s])
                byshift[-s] = keep(x, d >= lim[s])
            for ta in range(3):
                at = i + (ta - 1) * r + extra
                for tb in range(3):
                    tap = (3 * ta + tb) * ch
                    gtaps[at, tap : tap + ch, :] = turn(byshift[tb - ta], tb)
        return carry

    lax.fori_loop(0, n // 16, grads_step, 0)

    for p in range(SLOT):
        loose = p + SLOT * ((lane16 - p + EDGE) >> 4)
        row = (loose & (n - 1)).astype(f32).astype(bf16)
        e = (lane16 - loose).astype(f32).astype(bf16)
        x = gedge[p]
        zero = jnp.array(0, bf16)
        for ta in range(3):
            at = packs + ((p + (ta - 1) * r) & (SLOT - 1))
            for tb in range(3):
                s = tb - ta
                tap = (3 * ta + tb) * ch
                if s == 0:
                    gtaps[at, tap : tap + ch, :] = jnp.zeros((ch, n), bf16)
                    continue
                if s > 0:
                    mask = (e < zero) & (e >= lim[-s])
                else:
                    mask = (e >= zero) & (e < lim[-s])
                if ta == 0:
                    mask = mask & (row >= lim[1])
                elif ta == 2:
                    mask = mask & (row < top[1])
                gtaps[at, tap : tap + ch, :] = turn(keep(x, mask), tb)

    for y in range(extra):
        for ta, i in ((0, y), (2, n - 1 - y)):

            @pl.when(r > y)
            def _(ta=ta, i=i):
                x = gz[i]
                d = ((lane16 - i) & (n - 1)).astype(f32).astype(bf16)
                at = xhalo + (i - r + extra if ta == 0 else extra + i + r - n)
                for tb in range(3):
                    s = tb - ta
                    if s == 0:
                        continue
                    mask = d >= top[s] if s > 0 else d < lim[-s]
                    tap = (3 * ta + tb) * ch
                    gtaps[at, tap : tap + ch, :] = turn(keep(x, mask), tb)

    taps_w = [kernel[t // 3, t % 3] for t in range(9)]
    w_out = jnp.concatenate(taps_w, axis=1)
    w_in = jnp.concatenate([w.astype(f32).T.astype(bf16) for w in taps_w], axis=1)
    kacc[...] = jnp.zeros(kacc.shape, f32)
    shift_by = jnp.broadcast_to(bias[...], (ch, n))

    def conv_step(g, carry):
        base = pl.multiple_of(g * 16, 16)
        done = []
        total = None
        for u in range(0, 16, 2):
            i = base + u
            both = jnp.concatenate([taps[i + EDGE], taps[i + EDGE + 1]], axis=1)
            grads = jnp.concatenate([gz[i], gz[i + 1]], axis=1)
            z = jnp.dot(w_out, both, preferred_element_type=f32)
            part = lax.dot_general(
                both, grads, (((1,), (1,)), ((), ())), preferred_element_type=f32
            )
            total = part if total is None else total + part
            for w in range(2):
                v = vmask[i + w + extra].astype(f32)[:8]
                y = hid[i + w] + (z[:, w * n : (w + 1) * n] + shift_by).reshape(sub, 8, n)
                y = (y * v[None]).reshape(ch, n).astype(bf16)
                done.append(pltpu.roll(y, (n - i - w) & (n - 1), 1))
        kacc[...] += total
        pair_out[:, pl.ds(base, 16), :] = jnp.swapaxes(jnp.stack(done), 0, 1)
        return carry

    lax.fori_loop(0, n // 16, conv_step, 0)

    accs[...] = jnp.zeros(accs.shape, f32)

    def spreads(at):
        both = jnp.concatenate([gtaps[at], gtaps[at + 1]], axis=1)
        da = jnp.dot(w_in, both, preferred_element_type=f32)
        return [
            slope[at + w] * da[:, w * n : (w + 1) * n].reshape(sub, 8, n) for w in range(2)
        ]

    def back_step(g, carry):
        base = g * group
        racc, c0, c1, bacc = accs[1], accs[4], accs[5], accs[7]
        for u in range(0, group, 2):
            i = base + u
            for w, dx in enumerate(spreads(i + extra)):
                gg = gz[i + w].astype(f32).reshape(sub, 8, n)
                bacc = bacc + gg
                dx = dx + gg
                racc = racc + jnp.where(
                    (lane8 == i + w)[None], jnp.sum(dx, axis=2, keepdims=True), 0.0
                )
                here = (lane8 >= i + w)[None]
                c0 = c0 + jnp.where(here, dx, 0.0)
                c1 = c1 + jnp.where(here, 0.0, dx)
        accs[1], accs[4], accs[5], accs[7] = racc, c0, c1, bacc
        return carry

    lax.fori_loop(0, n // group, back_step, 0)

    def add_columns(dx, t):
        for b in range(4):
            accs[3 + b] += jnp.where((t == b - 1)[None], dx, 0.0)

    for y in range(0, 2 * extra, 2):
        i0 = near_rows[y]
        for w, dx in enumerate(spreads(i0 + extra)):
            i = i0 + w
            add_columns(dx, (i + ((lane8 - i) & (n - 1))) >> 7)
            total = jnp.sum(dx, axis=2, keepdims=True)
            accs[0 if y < extra else 2] += jnp.where((lane8 == (i & (n - 1)))[None], total, 0.0)
        for w, dx in enumerate(spreads(xhalo + y)):
            i = i0 + w
            e = ((lane8 - i + EDGE) & (n - 1)) - EDGE
            d = jnp.where(e < 0, e, e + n)
            add_columns(dx, (i + d) >> 7)
            total = jnp.sum(dx, axis=2, keepdims=True)
            accs[0 if y < extra else 2] += jnp.where((lane8 == (i & (n - 1)))[None], total, 0.0)
    for p in range(0, SLOT, 2):
        for w, dx in enumerate(spreads(packs + p)):
            q = p + w
            loose = q + SLOT * ((lane8 - q + EDGE) >> 4)
            e = lane8 - loose
            d = jnp.where(e < 0, e, e + n)
            add_columns(dx, ((loose & (n - 1)) + d) >> 7)
            x = dx.reshape(ch, n)
            for step in (1, 2, 4, 8):
                x = x + pltpu.roll(x, n - step, 1)
            x = pltpu.roll(x, EDGE, 1).reshape(sub, 8, n)
            accs[1] += jnp.where(((lane8 & (SLOT - 1)) == q)[None], x, 0.0)

    sums[...] = jnp.zeros(sums.shape, f32)
    for t in range(3):
        at = r_id + t - 1

        @pl.when((at >= 0) & (at < blocks))
        def _(at=at, t=t):
            sums[at, :ch, :] = accs[t].reshape(ch, n)

    for t in range(4):
        at = r_id + k_id + t - 1

        @pl.when((at >= 0) & (at < blocks))
        def _(at=at, t=t):
            sums[at, ch:, :] = accs[3 + t].reshape(ch, n)

    full = jnp.concatenate(
        [kacc[...].T, jnp.zeros((ch, 3 * n - 9 * ch), f32)], axis=1
    )
    lanes = lax.broadcasted_iota(jnp.int32, (ch, 3 * n), 1)
    btotal = jnp.sum(accs[7].reshape(ch, n), axis=1, keepdims=True)
    full = jnp.where(lanes == 9 * ch, btotal, full)
    for t in range(3):
        kgrad[t * ch : (t + 1) * ch, :] = full[:, t * n : (t + 1) * n]


def tile_call(gathered, kernel, bias, cot, dil, band):
    blocks, _, n = gathered.shape
    ch = bias.shape[0]
    sub = ch // 8
    f32, bf16 = jnp.float32, jnp.bfloat16
    vmem = pl.BlockSpec(memory_space=pltpu.VMEM)
    smem = pl.BlockSpec(memory_space=pltpu.SMEM)
    units = n + 4 * MAXDIL + SLOT
    return pl.pallas_call(
        tile_kernel,
        out_shape=(
            jax.ShapeDtypeStruct((ch, n, n), bf16),
            jax.ShapeDtypeStruct((blocks, 2 * ch, n), f32),
            jax.ShapeDtypeStruct((3 * ch, n), f32),
        ),
        in_specs=[vmem, vmem, vmem, vmem, smem, smem],
        out_specs=(vmem, vmem, vmem),
        scratch_shapes=[
            pltpu.VMEM((SLOT + 2 * MAXDIL, ch, n), bf16),
            pltpu.VMEM((n + 2 * EDGE, 9 * ch, n), bf16),
            pltpu.VMEM((units, 9 * ch, n), bf16),
            pltpu.VMEM((n, sub, 8, n), f32),
            pltpu.VMEM((units, sub, 8, n), f32),
            pltpu.VMEM((units, 16, n), bf16),
            pltpu.VMEM((n, ch, n), bf16),
            pltpu.VMEM((SLOT, ch, n), bf16),
            pltpu.VMEM((4, sub, 8, n), f32),
            pltpu.VMEM((4, 8, n), f32),
            pltpu.VMEM((8, sub, 8, n), f32),
            pltpu.VMEM((9 * ch, ch), f32),
        ],
        compiler_params=pltpu.CompilerParams(vmem_limit_bytes=60 * 1024 * 1024),
    )(gathered, kernel, bias.reshape(ch, 1), cot, dil, band)


def swapped(value, axis, bit):
    return lax.ppermute(value, axis, [(i, i ^ bit) for i in range(lax.axis_size(axis))])


def local(emb_rows, emb_cols, kernel, bias, cotangent, valid, dilation, band):
    ch, n = emb_rows.shape
    row_devices, diag_devices = lax.axis_size("row"), lax.axis_size("diag")
    assert cotangent.shape[2] == n == 128
    assert row_devices & (row_devices - 1) == 0 and diag_devices & (diag_devices - 1) == 0
    total_diags = n * diag_devices
    known = jnp.broadcast_to(valid.astype(jnp.bfloat16)[None], (16, n))
    bins = jnp.concatenate([emb_cols, emb_rows, known], axis=0)
    gathered = lax.all_gather(bins, "row")
    pair_out, sums, kgrad = tile_call(gathered, kernel, bias, cotangent, dilation, band)

    place = lax.axis_index("row")
    bit = row_devices // 2
    while bit:
        halves = sums.reshape((2, bit) + sums.shape[1:])
        mine = (place // bit) & 1
        kept = lax.dynamic_index_in_dim(halves, mine, 0, False)
        sent = lax.dynamic_index_in_dim(halves, 1 - mine, 0, False)
        came = swapped(jnp.concatenate([sent.reshape(-1, n), kgrad], axis=0), "row", bit)
        sums = kept + came[: bit * 2 * ch].reshape(kept.shape)
        kgrad = kgrad + came[bit * 2 * ch :]
        bit //= 2
    both = jnp.concatenate([sums.reshape(2 * ch, n), kgrad], axis=0)
    bit = 1
    while bit < diag_devices:
        both = both + swapped(both, "diag", bit)
        bit *= 2
    embed_scale = 1.0 / jnp.sqrt(jnp.float32(total_diags))
    weight_scale = 1.0 / jnp.sqrt(jnp.float32(row_devices * n) * jnp.float32(total_diags))
    wide = both[2 * ch :].reshape(3, ch, n).transpose(1, 0, 2).reshape(ch, 3 * n)
    kernel_grad = wide[:, : 9 * ch].reshape(ch, 9, ch).transpose(1, 0, 2).reshape(3, 3, ch, ch)
    return (
        pair_out,
        both[:ch] * embed_scale,
        both[ch : 2 * ch] * embed_scale,
        kernel_grad * weight_scale,
        wide[:, 9 * ch] * weight_scale,
    )


def solution(mesh):
    in_specs = (
        P(None, ("grp", "row")),
        P(None, ("grp", "row")),
        P(),
        P(),
        P(None, ("grp", "row"), "diag"),
        P(("grp", "row")),
        P("grp"),
        P("grp"),
    )
    out_specs = (
        P(None, ("grp", "row"), "diag"),
        P(None, ("grp", "row")),
        P(None, ("grp", "row")),
        P("grp", None, None, None),
        P("grp"),
    )
    return jax.shard_map(local, mesh=mesh, in_specs=in_specs, out_specs=out_specs, check_vma=False)
```

time: 240 us -> 58.1 us (0.24)
  blocking collectives: 99.2 us -> 6.72 us
  local copies, waits for them, and re-layouts: 63.4 us -> 3.15 us
  starting transfers between devices: 37.8 us -> 6.83 us
  Pallas kernels: 0 us -> 27.2 us
  matrix products: 20.6 us -> 0 us
  other arithmetic: 12.9 us -> 1.24 us
  waiting for transfers between devices: 1.79 us -> 10.6 us
    psum x2 -> x0, blocking collectives: 99.2 us -> none  [the longest x1 80.3 us: local(): lax.psum((kernel_portion, bias_part), ('row', 'diag'))]
    ppermute x21 -> x4, starting transfers between devices: 37.8 us -> 6.83 us  [swapped(): lax.ppermute(value, axis, [(i, i ^ bit) for i in range(lax.axis_size(axis...]
    pallas_call x0 -> x1, Pallas kernels: none -> 27.2 us  [tile_call(): pl.pallas_call(tile_kernel, out_shape=(jax.ShapeDtypeStruct((ch, n, n), b...]
    reshape x4 -> x2, local copies, waits for them, and re-layouts: 23.2 us -> 0.7 us  [the longest x1 0.69 us: tile_call(): bias.reshape(ch, 1)]
    dot_general x27 -> x0, matrix products: 20.6 us -> none  [contract(): return jnp.einsum(form, left, right, preferred_element_type=jnp.float32)]
    slice x12 -> x2, local copies, waits for them, and re-layouts: 14 us -> 0.01 us  [the longest x1 0.01 us: local(): sums = kept + came[:bit * 2 * ch].reshape(kept.shape)]
    unnamed x35 -> x12, local copies, waits for them, and re-layouts: 10.7 us -> 0.68 us
    ppermute x21 -> x4, waiting for transfers between devices: 1.79 us -> 10.6 us  [swapped(): lax.ppermute(value, axis, [(i, i ^ bit) for i in range(lax.axis_size(axis...]
  transfers between devices with their start and end apart: 21 -> 4, of which waited for: 1 -> 4; matrix products, arithmetic and copies ran while one was open for 22% -> 0% of each run, Pallas kernels for 0% -> 0%
where the time goes in v1:
time: 58.1 us; the launch traced here: 57.8 us
  Pallas kernels  27.2 us (47%)
  waiting for transfers between devices  10.6 us (18%)
  starting transfers between devices  6.83 us (12%)
  blocking collectives  6.72 us (12%)
  local copies, waits for them, and re-layouts  3.15 us (5%)
  between operations  2.08 us (4%)
  other arithmetic  1.24 us (2%)
    pallas_call x1, Pallas kernels, tile_call(): pl.pallas_call(tile_kernel, out_shape=(jax.ShapeDtypeStruct((ch, n, n), b...  27.2 us
    ppermute x4, waiting for transfers between devices, swapped(): lax.ppermute(value, axis, [(i, i ^ bit) for i in range(lax.axis_size(axis...  10.6 us
    ppermute x4, starting transfers between devices, swapped(): lax.ppermute(value, axis, [(i, i ^ bit) for i in range(lax.axis_size(axis...  6.83 us
    all_gather x1, blocking collectives, local(): gathered = lax.all_gather(bins, 'row')  6.72 us
  transfers between devices with their start and end apart: 4, of which 4 were waited for; matrix products, arithmetic and copies ran while one was open for 0% of the time, Pallas kernels for 0%

profile of v1, /device:TPU:0, one launch (start us, length us, event | category | flops | bytes accessed | tf_op | source)
XLA Modules:
  0.0 57.8 jit_solution(12402801445169685209)
XLA Ops:
  1.3 0.0 copy-start.5
  2.0 0.0 copy-done.5
  2.0 0.0 copy-start.4
  2.0 0.6 %copy-done.4 = f32[32]{0:T(128)S(1)} copy-done((f32[32]{0:T(128)S(1)}, f32[32]{0:T(128)}, u32[]{:S(2)}) %copy-start.4) | copy-done | bytes 152
  2.6 0.0 copy-start.2
  2.6 0.0 copy-start.3
  2.6 0.7 %copy.13.bias = f32[32,1]{1,0:T(8,128)} copy(f32[32,1]{0,1:T(1,128)S(1)} %bitcast.31) | data formatting | bytes 256 | tf_op jit(solution)/shard_map/reshape | solution.py:388
  3.3 0.0 copy-done.2
  3.3 0.0 copy-done.3
  3.4 6.7 %all-gather = bf16[320,128]{1,0:T(8,128)(2,1)} all-gather(bf16[80,128]{1,0:T(8,128)(2,1)S(1)} %pad_maximum_fusion.3), channel_id=2, replica_groups=mesh['grp'=2,'row'=4,'diag'=4] {'row'}, dimensions={0}, use_global_device_ids=true | all-gather | bytes 102400 | tf_op jit(solution)/shard_map/all_gather | solution.py:403
  10.1 27.2 %shard_map.119 = (bf16[32,128,128]{2,1,0:T(8,128)(2,1)}, f32[4,64,128]{2,1,0:T(8,128)}, f32[96,128]{1,0:T(8,128)}) custom-call(bf16[4,80,128]{2,1,0:T(8,128)(2,1)} %bitcast.24, bf16[3,3,32,32]{3,2,1,0:T(8,128)(2,1)} %kernel.1, f32[32,1]{1,0:T(8,128)} %copy.13.bias, bf16[32,128,128]{2,1,0:T(8,128)(2,1)} %cot.1, s32[1]{0:T(128)S(6)} %copy.16.dil, s32[1]{0:T(128)S(6)} %copy.17.band), custom_call_target="tpu_custom_call" | custom-call | tf_op jit(solution)/shard_map/pallas_call | solution.py:364
  37.2 0.0 copy-start
  37.2 0.9 %constant_dynamic-slice_fusion = f32[1,2,64,128]{3,2,1,0:T(8,128)S(1)} fusion(f32[2,2,64,128]{3,2,1,0:T(8,128)} %bitcast.29, s32[]{:T(128)S(6)} %select_n.22), kind=kLoop, calls=%fused_computation.12 | loop fusion | bytes 131076 | tf_op jit(solution)/shard_map/jit(dynamic_index_in_dim)/dynamic_slice | solution.py:412
  38.1 0.0 copy-done
  38.1 0.0 copy-start.1
  38.1 2.1 %collective-permute-start = (f32[224,128]{1,0:T(8,128)S(1)}, f32[224,128]{1,0:T(8,128)S(1)}, u32[]{:S(2)}, u32[]{:S(2)}) collective-permute-start(f32[224,128]{1,0:T(8,128)S(1)} %pad_maximum_fusion), channel_id=1, source_target_pairs={{0,8},{4,12},{8,0},{12,4},{1,9},{5,13},{9,1},{13,5},{2,10},{6,14},... | collective-permute-start | bytes 344072 | tf_op jit(solution)/shard_map/ppermute | solution.py:392
  40.2 3.6 %collective-permute-done = f32[224,128]{1,0:T(8,128)S(1)} collective-permute-done((f32[224,128]{1,0:T(8,128)S(1)}, f32[224,128]{1,0:T(8,128)S(1)}, u32[]{:S(2)}, u32[]{:S(2)}) %collective-permute-start) | collective-permute-done | bytes 114720 | tf_op jit(solution)/shard_map/ppermute | solution.py:392
  43.8 0.0 copy-done.1
  43.9 0.1 collective-permute-start.1
  44.0 1.3 %collective-permute-done.1 = f32[160,128]{1,0:T(8,128)S(1)} collective-permute-done((f32[160,128]{1,0:T(8,128)S(1)}, f32[160,128]{1,0:T(8,128)S(1)}, u32[]{:S(2)}, u32[]{:S(2)}) %collective-permute-start.1) | collective-permute-done | bytes 81952 | tf_op jit(solution)/shard_map/ppermute | solution.py:392
  45.3 1.9 %collective-permute-start.2 = (f32[160,128]{1,0:T(8,128)S(1)}, f32[160,128]{1,0:T(8,128)S(1)}, u32[]{:S(2)}, u32[]{:S(2)}) collective-permute-start(f32[160,128]{1,0:T(8,128)S(1)} %pad_maximum_fusion.2), channel_id=1, source_target_pairs={{0,1},{1,0},{2,3},{3,2},{4,5},{5,4},{6,7},{7,6},{8,9},{9,8},{10,11... | collective-permute-start | bytes 245768 | tf_op jit(solution)/shard_map/ppermute | solution.py:392
  47.2 2.8 %collective-permute-done.2 = f32[160,128]{1,0:T(8,128)S(1)} collective-permute-done((f32[160,128]{1,0:T(8,128)S(1)}, f32[160,128]{1,0:T(8,128)S(1)}, u32[]{:S(2)}, u32[]{:S(2)}) %collective-permute-start.2) | collective-permute-done | bytes 81952 | tf_op jit(solution)/shard_map/ppermute | solution.py:392
  50.0 2.8 %collective-permute-start.3 = (f32[160,128]{1,0:T(8,128)S(1)}, f32[160,128]{1,0:T(8,128)S(1)}, u32[]{:S(2)}, u32[]{:S(2)}) collective-permute-start(f32[160,128]{1,0:T(8,128)S(1)} %fusion.1), channel_id=1, source_target_pairs={{0,2},{1,3},{2,0},{3,1},{4,6},{5,7},{6,4},{7,5},{8,10},{9,11},{10,... | collective-permute-start | bytes 245768 | tf_op jit(solution)/shard_map/ppermute | solution.py:392
  52.8 3.0 %collective-permute-done.3 = f32[160,128]{1,0:T(8,128)S(1)} collective-permute-done((f32[160,128]{1,0:T(8,128)S(1)}, f32[160,128]{1,0:T(8,128)S(1)}, u32[]{:S(2)}, u32[]{:S(2)}) %collective-permute-start.3) | collective-permute-done | bytes 81952 | tf_op jit(solution)/shard_map/ppermute | solution.py:392
  55.8 0.6 %slice_multiply_fusion.1 = (f32[32,128]{1,0:T(8,128)}, f32[32,128]{1,0:T(8,128)}) fusion(f32[160,128]{1,0:T(8,128)S(1)} %add.46), kind=kLoop, calls=%fused_computation.10 | loop fusion | flops 8192 | bytes 65536 | tf_op jit(solution)/shard_map/mul | solution.py:429
  56.4 0.1 copy.14
  56.5 0.5 fusion
  57.0 0.8 %copy.15 = f32[32,9,32]{2,0,1:T(8,128)} copy(f32[32,9,32]{0,2,1:T(8,128)S(1)} %bitcast.23) | data formatting | bytes 73728 | tf_op jit(solution)/shard_map/mul | solution.py:430
  (16 shorter events, 0.1 us)
Async XLA Ops:
  1.3 0.7 %copy-start.5 = (s32[128]{0:T(128)S(1)}, s32[128]{0:T(128)}, u32[]{:S(2)}) copy-start(s32[128]{0:T(128)} %param.13) | copy-start | bytes 1540
  2.0 0.7 %copy-start.4 = (f32[32]{0:T(128)S(1)}, f32[32]{0:T(128)}, u32[]{:S(2)}) copy-start(f32[32]{0:T(128)} %param.11) | copy-start | bytes 388
  2.6 0.7 %copy-start.2 = (bf16[32,128]{1,0:T(8,128)(2,1)S(1)}, bf16[32,128]{1,0:T(8,128)(2,1)}, u32[]{:S(2)}) copy-start(bf16[32,128]{1,0:T(8,128)(2,1)} %param.8) | copy-start | bytes 24580
  2.6 0.7 %copy-start.3 = (bf16[32,128]{1,0:T(8,128)(2,1)S(1)}, bf16[32,128]{1,0:T(8,128)(2,1)}, u32[]{:S(2)}) copy-start(bf16[32,128]{1,0:T(8,128)(2,1)} %param.9) | copy-start | bytes 24580
  37.2 0.9 %copy-start = (f32[96,128]{1,0:T(8,128)S(1)}, f32[96,128]{1,0:T(8,128)}, u32[]{:S(2)}) copy-start(f32[96,128]{1,0:T(8,128)} %get-tuple-element.10) | copy-start | bytes 147460
  38.1 5.7 %copy-start.1 = (f32[4,64,128]{2,1,0:T(8,128)S(1)}, f32[4,64,128]{2,1,0:T(8,128)}, u32[]{:S(2)}) copy-start(f32[4,64,128]{2,1,0:T(8,128)} %get-tuple-element.9) | copy-start | bytes 393220
  38.1 5.7 %collective-permute-start = (f32[224,128]{1,0:T(8,128)S(1)}, f32[224,128]{1,0:T(8,128)S(1)}, u32[]{:S(2)}, u32[]{:S(2)}) collective-permute-start(f32[224,128]{1,0:T(8,128)S(1)} %pad_maximum_fusion), channel_id=1, source_target_pairs={{0,8},{4,12},{8,0},{12,4},{1,9},{5,13},{9,1},{13,5},{2,10},{6,14},... | collective-permute-start | bytes 344072 | tf_op jit(solution)/shard_map/ppermute | solution.py:392
  43.9 1.3 %collective-permute-start.1 = (f32[160,128]{1,0:T(8,128)S(1)}, f32[160,128]{1,0:T(8,128)S(1)}, u32[]{:S(2)}, u32[]{:S(2)}) collective-permute-start(f32[160,128]{1,0:T(8,128)S(1)} %pad_maximum_fusion.1), channel_id=1, source_target_pairs={{0,4},{4,0},{8,12},{12,8},{1,5},{5,1},{9,13},{13,9},{2,6},{6,2},{1... | collective-permute-start | bytes 245768 | tf_op jit(solution)/shard_map/ppermute | solution.py:392
  45.3 4.6 %collective-permute-start.2 = (f32[160,128]{1,0:T(8,128)S(1)}, f32[160,128]{1,0:T(8,128)S(1)}, u32[]{:S(2)}, u32[]{:S(2)}) collective-permute-start(f32[160,128]{1,0:T(8,128)S(1)} %pad_maximum_fusion.2), channel_id=1, source_target_pairs={{0,1},{1,0},{2,3},{3,2},{4,5},{5,4},{6,7},{7,6},{8,9},{9,8},{10,11... | collective-permute-start | bytes 245768 | tf_op jit(solution)/shard_map/ppermute | solution.py:392
  50.0 5.8 %collective-permute-start.3 = (f32[160,128]{1,0:T(8,128)S(1)}, f32[160,128]{1,0:T(8,128)S(1)}, u32[]{:S(2)}, u32[]{:S(2)}) collective-permute-start(f32[160,128]{1,0:T(8,128)S(1)} %fusion.1), channel_id=1, source_target_pairs={{0,2},{1,3},{2,0},{3,1},{4,6},{5,7},{6,4},{7,5},{8,10},{9,11},{10,... | collective-permute-start | bytes 245768 | tf_op jit(solution)/shard_map/ppermute | solution.py:392

commit v2 on v1

v2 whole, which is shorter than its diff:
```python
import jax
import jax.numpy as jnp
from jax import lax
from jax.experimental import pallas as pl
from jax.experimental.pallas import tpu as pltpu
from jax.sharding import PartitionSpec as P

MAXDIL = 4
EDGE = 2 * MAXDIL
SLOT = 2 * EDGE
GELU_C = 0.7978845608028654
GELU_A = 0.044715
WORD_BITS = 6
VMEM_LIMIT = (65472 - 900) * 1024
OUT_LIMIT = (65472 - 1500) * 1024


def gelu_and_slope(h):
    square = h * h
    t = jnp.tanh(h * (GELU_C + (GELU_C * GELU_A) * square))
    half = 0.5 * h
    one = 1.0 + t
    slope = 0.5 * one + half * (1.0 - t * t) * (GELU_C + (3.0 * GELU_C * GELU_A) * square)
    return half * one, slope


def crossings():
    return [(ta, tb) for ta in range(3) for tb in range(3) if ta != tb]


def pack_kernel(emb_cols, emb_rows, valid, dil, band, kernel, bins, weights):
    f32, bf16 = jnp.float32, jnp.bfloat16
    ch, n = emb_cols.shape
    bins[:ch] = emb_cols[...]
    bins[ch : 2 * ch] = emb_rows[...]
    known = jnp.broadcast_to(valid[...].astype(f32), (8, n))
    wide = jnp.broadcast_to(band[...], (8, n))
    line = lax.broadcasted_iota(jnp.int32, (8, n), 0)
    settings = jnp.where(line == 1, wide >> WORD_BITS, wide & (2**WORD_BITS - 1))
    settings = jnp.where(line == 0, jnp.broadcast_to(dil[...], (8, n)), settings)
    bins[2 * ch :] = jnp.concatenate([known, settings.astype(f32)], axis=0).astype(bf16)
    taps = [kernel[t // 3, t % 3] for t in range(9)]
    turned = [w.astype(f32).T.astype(bf16) for w in taps]
    cross = [3 * ta + tb for ta, tb in crossings()]
    weights[0] = jnp.concatenate(taps, axis=1)
    weights[1] = jnp.concatenate(turned, axis=1)
    weights[2, :, : 6 * ch] = jnp.concatenate([taps[t] for t in cross], axis=1)
    weights[3, :, : 6 * ch] = jnp.concatenate([turned[t] for t in cross], axis=1)


def pack_call(emb_cols, emb_rows, valid, dil, band, kernel):
    ch, n = emb_cols.shape
    vmem = pl.BlockSpec(memory_space=pltpu.VMEM)
    return pl.pallas_call(
        pack_kernel,
        out_shape=(
            jax.ShapeDtypeStruct((2 * ch + 16, n), jnp.bfloat16),
            jax.ShapeDtypeStruct((4, ch, 9 * ch), jnp.bfloat16),
        ),
        in_specs=[vmem] * 6,
        out_specs=(vmem, vmem),
        compiler_params=pltpu.CompilerParams(vmem_limit_bytes=65472 * 1024),
        name="pack",
    )(
        emb_cols, emb_rows, valid.reshape(1, n), dil.reshape(1, 1), band.reshape(1, 1), kernel
    )


def tile_kernel(
    gathered, weights, cot_hbm,
    kept, sent, act_hbm, held_hbm,
    act, held, grd, slope, halo, edge, gedge, dfix, cols, colv, accs, kacc, kedge,
    place, nears, cot, sems,
):
    cot_in = pltpu.make_async_copy(cot_hbm, cot, sems.at[0])
    cot_in.start()
    ch = cot.shape[0]
    n = cot.shape[1]
    sub = ch // 8
    blocks = gathered.shape[0]
    extra = MAXDIL
    ext = n + 2 * extra
    packs = ext
    xhalo = ext + SLOT
    r_id = lax.axis_index("row")
    k_id = lax.axis_index("diag")
    settings = gathered[r_id, 2 * ch + 8 : 2 * ch + 16, :].astype(jnp.float32)
    r, high, rest = [jnp.max(settings[j : j + 1, :]).astype(jnp.int32) for j in range(3)]
    width = (high << WORD_BITS) + rest - k_id * n
    low = -k_id * n
    f32, bf16 = jnp.float32, jnp.bfloat16
    lane8 = lax.broadcasted_iota(jnp.int32, (8, n), 1)
    lane16 = lax.broadcasted_iota(jnp.int32, (16, n), 1)

    def small(x):
        return x.astype(f32).astype(bf16)

    reach = {s: small(s * r) for s in (1, 2, -1, -2)}
    zero = jnp.array(0, bf16)

    def block_of(index, first, count):
        found = gathered[jnp.clip(index, 0, blocks - 1), first : first + count, :]
        inside = ((index >= 0) & (index < blocks)).astype(f32)
        return found.astype(f32) * inside

    for t in range(4):
        cols[t] = block_of(r_id + k_id + t - 1, 0, ch).reshape(sub, 8, n)
        colv[t] = block_of(r_id + k_id + t - 1, 2 * ch, 8)

    tall = ch + 16

    def row_values(index):
        return block_of(index, ch, tall)

    own = row_values(r_id)
    own16 = own.astype(bf16)
    sublane = lax.broadcasted_iota(jnp.int32, (16, n), 0)
    ones = [(sublane == u).astype(f32).astype(bf16) for u in range(16)]
    ones = jnp.concatenate(ones, axis=1)

    def spread16(rows):
        wide = jnp.dot(rows[:, :16], ones, preferred_element_type=f32)
        parts = [wide[:, u * n : (u + 1) * n] for u in range(16)]
        return [(x[:ch].reshape(sub, 8, n), x[ch : ch + 8]) for x in parts]

    def unit(slot, rows, rows_v, col, col_v, inside):
        v = jnp.where(inside, rows_v * col_v, 0.0)
        h = (rows + col) * v[None]
        a, g = gelu_and_slope(h)
        slope[slot] = g * v[None]
        return v, h, a.reshape(ch, n).astype(bf16)

    def pick(t):
        col, col_v = cols[3], colv[3]
        for b in (2, 1, 0):
            here = t == b - 1
            col = jnp.where(here[None], cols[b], col)
            col_v = jnp.where(here, colv[b], col_v)
        return col, col_v

    def half(x):
        return x.reshape(2, 16, n)

    def keep(x, mask):
        return jnp.where(mask[None], half(x), jnp.zeros((2, 16, n), bf16)).reshape(ch, n)

    def turns(x, back):
        ahead, behind = pltpu.roll(x, r, 1), pltpu.roll(x, n - r, 1)
        return (behind, x, ahead) if back else (ahead, x, behind)

    def store_turns(ref, at, x, back):
        for tb, y in enumerate(turns(x, back)):
            ref[at, tb * ch : (tb + 1) * ch, :] = y

    def pack_lanes(lanes, p):
        loose = p + SLOT * ((lanes - p + EDGE) >> 4)
        return loose & (n - 1), lanes - loose

    lane1 = lax.broadcasted_iota(jnp.int32, (8, n), 1)
    whole = lax.broadcasted_iota(jnp.int32, (n, n), 0)

    def packs_step(g, carry):
        for two in range(2):
            p0 = 4 * g + 2 * two
            rows_at = [pack_lanes(lane1, p0 + w)[0][:1] for w in range(2)]
            to_row = jnp.concatenate(
                [(whole == x).astype(f32).astype(bf16) for x in rows_at], axis=1
            )
            place[2 * g + two] = to_row
            found = jnp.dot(own16, to_row, preferred_element_type=f32)
            for w in range(2):
                p = p0 + w
                row, e = pack_lanes(lane8, p)
                d = jnp.where(e < 0, e, e + n)
                col, col_v = pick((row + d) >> 7)
                mine = found[:, w * n : (w + 1) * n]
                _, _, a = unit(
                    packs + p, mine[:ch].reshape(sub, 8, n), mine[ch : ch + 8], col, col_v,
                    (d >= low) & (d < width),
                )
                halo[p] = a
        return carry

    lax.fori_loop(0, SLOT // 4, packs_step, 0)

    for at in list(range(2 * extra)) + list(range(n + 2 * extra, n + 4 * extra)):
        grd[at] = jnp.zeros(grd.shape[1:], bf16)

    def rows_step(g, carry):
        base = pl.multiple_of(g * 16, 16)
        turned = pltpu.roll(own, (n - base) & (n - 1), 1).astype(bf16)
        for u, (rows, rows_v) in enumerate(spread16(turned)):
            i = base + u
            here = lane8 >= i
            col = jnp.where(here[None], cols[1], cols[2])
            col_v = jnp.where(here, colv[1], colv[2])
            d = (lane8 - i) & (n - 1)
            v, h, a = unit(i + extra, rows, rows_v, col, col_v, (d >= low) & (d < width))
            held[i, :ch, :] = h.reshape(ch, n)
            held[i, ch:, :] = v
            store_turns(act, i + extra, a, False)
        return carry

    lax.fori_loop(0, n // 16, rows_step, 0)

    def grads_step(g, carry):
        base = pl.multiple_of(g * 16, 16)
        block = jnp.swapaxes(cot[:, pl.ds(base, 16), :], 0, 1)
        for u in range(16):
            i = base + u
            v = held[i, ch:, :]
            v2 = jnp.concatenate([v, v], axis=0).astype(bf16)
            x = (half(pltpu.roll(block[u], i, 1)) * v2[None]).reshape(ch, n)
            store_turns(grd, i + 2 * extra, x, True)
        return carry

    held_out = pltpu.make_async_copy(
        held.at[pl.ds(0, n)], held_hbm.at[pl.ds(0, n)], sems.at[2]
    )
    held_out.start()
    cot_in.wait()
    lax.fori_loop(0, n // 16, grads_step, 0)

    def edges_step(p, carry):
        row = small(pack_lanes(lane16, p)[0])
        a = x = jnp.zeros((2, 16, n), bf16)
        for m in range(n // SLOT):
            i = p + m * SLOT
            here = (row == small(i))[None]
            a = jnp.where(here, half(act[i + extra, ch : 2 * ch, :]), a)
            x = jnp.where(here, half(grd[i + 2 * extra, ch : 2 * ch, :]), x)
        edge[p] = a.reshape(ch, n)
        gedge[p] = x.reshape(ch, n)
        return carry

    lax.fori_loop(0, SLOT, edges_step, 0)

    lane_tall = lax.broadcasted_iota(jnp.int32, (tall, n), 1)
    near = jnp.where(
        lane_tall < extra,
        pltpu.roll(row_values(r_id - 1), extra, 1),
        pltpu.roll(row_values(r_id + 1), extra, 1),
    )
    for y, (rows, rows_v) in enumerate(spread16(near.astype(bf16))[: 2 * extra]):
        nears[y, :sub] = rows
        nears[y, sub] = rows_v

    def near_row(y):
        return jnp.where(y < extra, y - extra, n + y - extra)

    def near_lanes(i):
        e = ((lane8 - i + EDGE) & (n - 1)) - EDGE
        return e, jnp.where(e < 0, e, e + n)

    def near_step(g, carry):
        for w in range(4):
            y = 4 * g + w
            i = near_row(y)
            rows, rows_v = nears[y, :sub], nears[y, sub]
            e, d = near_lanes(i)
            col, col_v = pick((i + d) >> 7)
            inside = (e < EDGE) & (d >= low) & (d < width)
            _, _, far = unit(xhalo + y, rows, rows_v, col, col_v, inside)
            d = (lane8 - i) & (n - 1)
            col, col_v = pick((i + d) >> 7)
            _, _, a = unit(i + extra, rows, rows_v, col, col_v, (d >= low) & (d < width))
            store_turns(act, i + extra, a, False)
            slot = (small((lane16 - i + EDGE) & (n - 1)) < jnp.array(SLOT, bf16))[None]
            q = i & (SLOT - 1)
            halo[SLOT + y] = jnp.where(slot, half(far), half(halo[q])).reshape(ch, n)
            edge[SLOT + y] = jnp.where(slot, half(a), half(edge[q])).reshape(ch, n)
        return carry

    lax.fori_loop(0, extra // 2, near_step, 0)
    act_out = pltpu.make_async_copy(act, act_hbm, sems.at[3])
    act_out.start()

    w_in = weights[1]
    w_out_edge, w_in_edge = weights[2, :, : 6 * ch], weights[3, :, : 6 * ch]
    crossing = crossings()
    kedge[...] = jnp.zeros(kedge.shape, f32)
    rows_last = small(n - r)

    def fix_taps(p):
        row, e = pack_lanes(lane16, p)
        row, e = small(row), small(e)
        found, wrong, away = [], [], []
        for ta in range(3):
            q = (p + (ta - 1) * r) & (SLOT - 1)
            at = q
            if ta == 0:
                at = jnp.where(p < r, q + extra, q)
            elif ta == 2:
                at = jnp.where(p + r >= SLOT, q + SLOT + extra, q)
            far, own_edge = turns(halo[at], False), turns(edge[at], False)
            back = turns(gedge[(p - (ta - 1) * r) & (SLOT - 1)], True)
            for tb in range(3):
                s = tb - ta
                if s == 0:
                    continue
                if s > 0:
                    mask = (e >= reach[-s]) & (e < zero)
                    spill = (e >= zero) & (e < reach[s])
                else:
                    mask = (e >= zero) & (e < reach[-s])
                    spill = (e >= reach[s]) & (e < zero)
                if ta == 0:
                    spill = spill & (row < rows_last)
                elif ta == 2:
                    spill = spill & (row >= reach[1])
                found.append(keep(far[tb], mask))
                wrong.append(keep(own_edge[tb], mask))
                away.append(keep(back[tb], spill))
        return [jnp.concatenate(x, axis=0) for x in (found, wrong, away)]

    def fix_pair(p):
        found, wrong, away = [
            jnp.concatenate(x, axis=1) for x in zip(fix_taps(p), fix_taps(p + 1))
        ]
        grads = jnp.concatenate([gedge[p], gedge[p + 1]], axis=1)
        z = jnp.dot(w_out_edge, found, preferred_element_type=f32) - jnp.dot(
            w_out_edge, wrong, preferred_element_type=f32
        )
        lanes = (((1,), (1,)), ((), ()))
        kedge[...] += lax.dot_general(
            found, grads, lanes, preferred_element_type=f32
        ) - lax.dot_general(wrong, grads, lanes, preferred_element_type=f32)
        da = jnp.dot(w_in_edge, away, preferred_element_type=f32)
        for w in range(2):
            held[n + p + w, :ch, :] = z[:, w * n : (w + 1) * n]
            dfix[p + w] = da[:, w * n : (w + 1) * n].reshape(sub, 8, n)

    def fix_step(g, carry):
        fix_pair(4 * g)
        fix_pair(4 * g + 2)
        return carry

    lax.fori_loop(0, SLOT // 4, fix_step, 0)
    fixes_out = pltpu.make_async_copy(
        held.at[pl.ds(n, SLOT)], held_hbm.at[pl.ds(n, SLOT)], sems.at[4]
    )
    fixes_out.start()

    for y in range(2 * extra):
        i = y - extra if y < extra else n + y - extra
        ta = 0 if y < extra else 2
        e = small(((lane16 - i + EDGE) & (n - 1)) - EDGE)
        parts = []
        for tb in range(3):
            s = tb - ta
            x = grd[i + (1 - ta) * r + 2 * extra, tb * ch : (tb + 1) * ch, :]
            if s > 0:
                parts.append(keep(x, (e >= zero) & (e < reach[s])))
            elif s < 0:
                parts.append(keep(x, (e >= reach[s]) & (e < zero)))
        first = 1 if ta == 0 else 6
        weights = w_in[:, first * ch : (first + 2) * ch]
        da = jnp.dot(weights, jnp.concatenate(parts, axis=0), preferred_element_type=f32)
        dfix[SLOT + y] = da.reshape(sub, 8, n)

    kacc[...] = jnp.zeros(kacc.shape, f32)
    accs[...] = jnp.zeros(accs.shape, f32)
    def spreads(i):
        both = two_rows(grd, i + 2 * extra, -r)
        da = jnp.dot(w_in, both, preferred_element_type=f32)
        return [da[:, w * n : (w + 1) * n].reshape(sub, 8, n) for w in range(2)]

    def kernel_part(i):
        both = jnp.concatenate([act[i + extra], act[i + extra + 1]], axis=1)
        grads = [
            jnp.concatenate(
                [grd[i + w + t * r + 2 * extra, ch : 2 * ch, :] for t in (1, 0, -1)], axis=0
            )
            for w in range(2)
        ]
        return lax.dot_general(
            both, jnp.concatenate(grads, axis=1), (((1,), (1,)), ((), ())),
            preferred_element_type=f32,
        )

    def back_step(g, carry):
        base = pl.multiple_of(g * 16, 16)
        total = None
        racc, c0, c1, bacc = accs[1], accs[4], accs[5], accs[7]
        for u in range(0, 16, 2):
            i = base + u
            part = kernel_part(i)
            total = part if total is None else total + part
            for w, da in enumerate(spreads(i)):
                slot = ((lane8 - (i + w) + EDGE) & (n - 1)) < SLOT
                da = da - jnp.where(slot[None], dfix[u + w], 0.0)
                gg = grd[i + w + 2 * extra, ch : 2 * ch, :].astype(f32).reshape(sub, 8, n)
                bacc = bacc + gg
                dx = gg + slope[i + w + extra] * da
                racc = racc + jnp.where(
                    (lane8 == i + w)[None], jnp.sum(dx, axis=2, keepdims=True), 0.0
                )
                here = (lane8 >= i + w)[None]
                c0 = c0 + jnp.where(here, dx, 0.0)
                c1 = c1 + jnp.where(here, 0.0, dx)
        accs[1], accs[4], accs[5], accs[7] = racc, c0, c1, bacc
        kacc[...] += total
        return carry

    lax.fori_loop(0, n // 16, back_step, 0)

    def add_columns(dx, t):
        for b in range(4):
            accs[3 + b] += jnp.where((t == b - 1)[None], dx, 0.0)

    def near_sums(g, carry):
        y0 = 2 * g
        i0 = near_row(y0)
        which = jnp.where(y0 < extra, 0, 2)
        for w, da in enumerate(spreads(i0)):
            i = i0 + w
            e, d = near_lanes(i)
            fix = dfix[SLOT + y0 + w]
            inner = slope[i + extra] * (da - fix)
            outer = slope[xhalo + y0 + w] * fix
            add_columns(inner, (i + ((lane8 - i) & (n - 1))) >> 7)
            add_columns(outer, (i + d) >> 7)
            total = jnp.sum(inner + outer, axis=2, keepdims=True)
            accs[which] += jnp.where((lane8 == (i & (n - 1)))[None], total, 0.0)
        kacc[...] += kernel_part(i0)
        return carry

    lax.fori_loop(0, extra, near_sums, 0)

    def pack_sums(g, carry):
        for two in range(2):
            dxs = []
            for w in range(2):
                p = 4 * g + 2 * two + w
                row, e = pack_lanes(lane8, p)
                dx = slope[packs + p] * dfix[p]
                add_columns(dx, (row + jnp.where(e < 0, e, e + n)) >> 7)
                dxs.append(dx.reshape(ch, n))
            rest = jnp.concatenate(dxs, axis=1)
            parts = []
            for _ in range(3):
                part = rest.astype(bf16)
                rest = rest - part.astype(f32)
                parts.append(part)
            found = lax.dot_general(
                jnp.concatenate(parts, axis=0), place[2 * g + two],
                (((1,), (1,)), ((), ())), preferred_element_type=f32,
            )
            total = found[:ch] + found[ch : 2 * ch] + found[2 * ch :]
            accs[1] += total.reshape(sub, 8, n)
        return carry

    lax.fori_loop(0, SLOT // 4, pack_sums, 0)

    half_blocks = blocks // 2
    mine = r_id // half_blocks
    kept[...] = jnp.zeros(kept.shape, f32)
    sent[...] = jnp.zeros(sent.shape, f32)

    def put(at, first, value):
        which = jnp.where(at >= half_blocks, 1, 0)
        slot = pl.multiple_of((at - which * half_blocks) * 2 * ch + first, ch)

        @pl.when((at >= 0) & (at < blocks) & (which == mine))
        def _():
            kept[pl.ds(slot, ch), :] = value

        @pl.when((at >= 0) & (at < blocks) & (which != mine))
        def _():
            sent[pl.ds(slot, ch), :] = value

    for t in range(3):
        put(r_id + t - 1, 0, accs[t].reshape(ch, n))
    for t in range(4):
        put(r_id + k_id + t - 1, ch, accs[3 + t].reshape(ch, n))

    parts = []
    for ta in range(3):
        part = kacc[:, ta * ch : (ta + 1) * ch]
        fixes = [
            kedge[crossing.index((ta, tb)) * ch : (crossing.index((ta, tb)) + 1) * ch, :]
            if ta != tb
            else jnp.zeros((ch, ch), f32)
            for tb in range(3)
        ]
        parts.append(part + jnp.concatenate(fixes, axis=0))
    full = jnp.concatenate(parts, axis=0).T
    full = jnp.concatenate([full, jnp.zeros((ch, 3 * n - 9 * ch), f32)], axis=1)
    lanes = lax.broadcasted_iota(jnp.int32, (ch, 3 * n), 1)
    btotal = jnp.sum(accs[7].reshape(ch, n), axis=1, keepdims=True)
    full = jnp.where(lanes == 9 * ch, btotal, full)
    for t in range(3):
        first = half_blocks * 2 * ch + t * ch
        sent[first : first + ch, :] = full[:, t * n : (t + 1) * n]
    held_out.wait()
    act_out.wait()
    fixes_out.wait()


def rows_of(ref, at, step):
    return jnp.concatenate([ref[at - step], ref[at], ref[at + step]], axis=0)


def two_rows(ref, at, step):
    return jnp.concatenate([rows_of(ref, at, step), rows_of(ref, at + 1, step)], axis=1)


def out_kernel(
    start, count, weights_hbm, bias_hbm, dil_hbm, act_hbm, held_hbm, *refs
):
    pair_out, weights, bias, act, held, done, dil, sems, act_sems, held_sems, done_sems = refs[-11:]
    f32, bf16 = jnp.float32, jnp.bfloat16
    ch, n = pair_out.shape[:2]
    sub = ch // 8

    def part(hbm, vmem, sem, first, there):
        rows = pl.ds(pl.multiple_of(first, 16), 16)
        return pltpu.make_async_copy(hbm.at[rows], vmem.at[pl.ds(there, 16)], sem)

    def act_part(g):
        return part(act_hbm, act, act_sems.at[g], (start + g) * 16, g * 16)

    def held_part(g):
        return part(held_hbm, held, held_sems.at[g], (start + g) * 16, g * 16)

    def done_part(g):
        rows = pl.ds(pl.multiple_of((start + g) * 16, 16), 16)
        return pltpu.make_async_copy(done.at[g], pair_out.at[:, rows, :], done_sems.at[g])

    fixes = part(held_hbm, held, held_sems.at[count], n, count * 16)
    small = [
        pltpu.make_async_copy(a, b, sems.at[j])
        for j, (a, b) in enumerate(
            ((dil_hbm, dil), (bias_hbm, bias), (weights_hbm.at[0], weights))
        )
    ]
    for copy in small:
        copy.start()
    fixes.start()
    act_part(0).start()
    for g in range(count):
        act_part(g + 1).start()
        held_part(g).start()
    lane8 = lax.broadcasted_iota(jnp.int32, (8, n), 1)
    for copy in small:
        copy.wait()
    w_out = weights[...]
    square = [lax.broadcasted_iota(jnp.int32, (ch, ch), x) for x in range(2)]
    shift_by = jnp.sum(
        jnp.where(square[0] == square[1], jnp.broadcast_to(bias[...], (ch, ch)), 0.0),
        axis=1, keepdims=True,
    )
    shift_by = jnp.broadcast_to(shift_by, (ch, n)).reshape(sub, 8, n)
    r = jnp.max(dil[...])
    fixes.wait()
    act_part(0).wait()

    def conv_step(g, carry):
        act_part(g + 1).wait()
        held_part(g).wait()
        found = []
        for u in range(0, 16, 2):
            k = g * 16 + u
            i = start * 16 + k
            z = jnp.dot(w_out, two_rows(act, k + MAXDIL, r), preferred_element_type=f32)
            for w in range(2):
                slot = ((lane8 - (i + w) + EDGE) & (n - 1)) < SLOT
                fix = held[count * 16 + u + w, :ch, :].reshape(sub, 8, n)
                y = (held[k + w, :ch, :] + z[:, w * n : (w + 1) * n]).reshape(sub, 8, n)
                y = y + shift_by + jnp.where(slot[None], fix, 0.0)
                y = (y * held[k + w, ch:, :][None]).reshape(ch, n).astype(bf16)
                found.append(pltpu.roll(y, (n - i - w) & (n - 1), 1))
        done[g] = jnp.swapaxes(jnp.stack(found), 0, 1)
        done_part(g).start()
        return carry

    lax.fori_loop(0, count, conv_step, 0)
    for g in range(count):
        done_part(g).wait()


def out_call(start, count, made, weights, bias, dil, act, held):
    _, ch3, n = act.shape
    ch = ch3 // 3
    hbm = pl.BlockSpec(memory_space=pltpu.HBM)
    dma = pltpu.SemaphoreType.DMA

    def body(*refs):
        out_kernel(start, count, *refs)

    return pl.pallas_call(
        body,
        out_shape=jax.ShapeDtypeStruct((ch, n, n), jnp.bfloat16),
        in_specs=[hbm] * (5 + len(made)),
        out_specs=hbm,
        input_output_aliases={5: 0} if made else {},
        scratch_shapes=[
            pltpu.VMEM(weights.shape[1:], weights.dtype),
            pltpu.VMEM((1, ch), jnp.float32),
            pltpu.VMEM((16 * (count + 1), ch3, n), act.dtype),
            pltpu.VMEM((16 * (count + 1), ch + 8, n), held.dtype),
            pltpu.VMEM((count, ch, 16, n), jnp.bfloat16),
            pltpu.VMEM((1, 1), jnp.int32),
            dma((3,)),
            dma((count + 1,)),
            dma((count + 1,)),
            dma((count,)),
        ],
        compiler_params=pltpu.CompilerParams(vmem_limit_bytes=OUT_LIMIT),
        cost_estimate=pl.CostEstimate(
            flops=288 * count * ch * ch * n, bytes_accessed=200 * count * ch * n, transcendentals=0
        ),
        name="outputs",
    )(weights, bias.reshape(1, ch), dil.reshape(1, 1), act, held, *made)


def tile_call(gathered, weights, cot):
    blocks, _, n = gathered.shape
    ch = cot.shape[0]
    assert blocks % 2 == 0
    sub = ch // 8
    f32, bf16 = jnp.float32, jnp.bfloat16
    vmem = pl.BlockSpec(memory_space=pltpu.VMEM)
    hbm = pl.BlockSpec(memory_space=pltpu.HBM)
    near = 2 * MAXDIL
    units = n + 2 * near + SLOT
    return pl.pallas_call(
        tile_kernel,
        out_shape=(
            jax.ShapeDtypeStruct((blocks * ch, n), f32),
            jax.ShapeDtypeStruct((blocks * ch + 3 * ch, n), f32),
            jax.ShapeDtypeStruct((n + SLOT, 3 * ch, n), bf16),
            jax.ShapeDtypeStruct((n + SLOT, ch + 8, n), f32),
        ),
        in_specs=[vmem, vmem, hbm],
        out_specs=(vmem, vmem, hbm, hbm),
        scratch_shapes=[
            pltpu.VMEM((n + SLOT, 3 * ch, n), bf16),
            pltpu.VMEM((n + SLOT, ch + 8, n), f32),
            pltpu.VMEM((n + 2 * near, 3 * ch, n), bf16),
            pltpu.VMEM((units, sub, 8, n), f32),
            pltpu.VMEM((SLOT + near, ch, n), bf16),
            pltpu.VMEM((SLOT + near, ch, n), bf16),
            pltpu.VMEM((SLOT, ch, n), bf16),
            pltpu.VMEM((SLOT + near, sub, 8, n), f32),
            pltpu.VMEM((4, sub, 8, n), f32),
            pltpu.VMEM((4, 8, n), f32),
            pltpu.VMEM((8, sub, 8, n), f32),
            pltpu.VMEM((3 * ch, 3 * ch), f32),
            pltpu.VMEM((6 * ch, ch), f32),
            pltpu.VMEM((SLOT // 2, n, 2 * n), bf16),
            pltpu.VMEM((near, sub + 1, 8, n), f32),
            pltpu.VMEM((ch, n, n), bf16),
            pltpu.SemaphoreType.DMA((5,)),
        ],
        compiler_params=pltpu.CompilerParams(vmem_limit_bytes=VMEM_LIMIT),
        cost_estimate=pl.CostEstimate(
            flops=54 * ch * ch * n * n, bytes_accessed=16 * ch * n * n, transcendentals=ch * n * n
        ),
        name="tile",
    )(gathered, weights, cot)


def final_kernel(scales, x, y, rows, cols, kgrad, bgrad):
    ch = rows.shape[0]
    n = rows.shape[1]
    total = x[...] + y[...]
    rows[...] = total[:ch] * scales[0]
    cols[...] = total[ch : 2 * ch] * scales[0]
    total = total[2 * ch :] * scales[1]
    for t in range(9):
        first, lane = (t * ch // n) * ch, t * ch % n
        kgrad[t] = total[first : first + ch, lane : lane + ch]
    first, lane = (9 * ch // n) * ch, 9 * ch % n
    part = jnp.broadcast_to(total[first : first + ch, lane : lane + 1], (ch, ch))
    square = [lax.broadcasted_iota(jnp.int32, (ch, ch), i) for i in range(2)]
    bgrad[...] = jnp.sum(jnp.where(square[0] == square[1], part, 0.0), axis=0, keepdims=True)


def final_call(x, y, embed_scale, weight_scale):
    n = x.shape[1]
    ch = x.shape[0] // 5
    f32 = jnp.float32

    def body(*refs):
        final_kernel((embed_scale, weight_scale), *refs)

    vmem = pl.BlockSpec(memory_space=pltpu.VMEM)
    return pl.pallas_call(
        body,
        out_shape=(
            jax.ShapeDtypeStruct((ch, n), f32),
            jax.ShapeDtypeStruct((ch, n), f32),
            jax.ShapeDtypeStruct((9, ch, ch), f32),
            jax.ShapeDtypeStruct((1, ch), f32),
        ),
        in_specs=[vmem, vmem],
        out_specs=(vmem,) * 4,
        compiler_params=pltpu.CompilerParams(vmem_limit_bytes=2 * 1024 * 1024),
        name="finish",
    )(x, y)


def swapped(value, axis, bit):
    return lax.ppermute(value, axis, [(i, i ^ bit) for i in range(lax.axis_size(axis))])


def local(emb_rows, emb_cols, kernel, bias, cotangent, valid, dilation, band):
    ch, n = emb_rows.shape
    row_devices, diag_devices = lax.axis_size("row"), lax.axis_size("diag")
    assert cotangent.shape[2] == n == 128
    assert row_devices & (row_devices - 1) == 0 and diag_devices & (diag_devices - 1) == 0
    total_diags = n * diag_devices
    bins, weights = pack_call(emb_cols, emb_rows, valid, dilation, band, kernel)
    gathered = lax.all_gather(bins, "row")
    kept, sent, *held = tile_call(gathered, weights, cotangent)
    groups = n // 16
    cut = groups - groups * 3 // 8
    made = ()

    place = lax.axis_index("row")
    bit = row_devices // 2
    while True:
        came = swapped(sent, "row", bit)
        if not made:
            made = (out_call(0, cut, (), weights, bias, dilation, *held),)
            came, *made = lax.optimization_barrier((came, *made))
        own = bit * 2 * ch
        sums, whole = kept + came[:own], sent[own:] + came[own:]
        bit //= 2
        if not bit:
            break
        halves = sums.reshape(2, bit * 2 * ch, n)
        mine = (place // bit) & 1
        kept = lax.dynamic_index_in_dim(halves, mine, 0, False)
        other = lax.dynamic_index_in_dim(halves, 1 - mine, 0, False)
        sent = jnp.concatenate([other, whole], axis=0)
    both = jnp.concatenate([sums, whole], axis=0)
    bit = 1
    while 2 * bit < diag_devices:
        both = both + swapped(both, "diag", bit)
        bit *= 2
    came = swapped(both, "diag", bit)
    pair_out = out_call(cut, groups - cut, tuple(made), weights, bias, dilation, *held)
    came, pair_out = lax.optimization_barrier((came, pair_out))
    rows, cols, kgrad, bgrad = final_call(
        both,
        came,
        1.0 / total_diags**0.5,
        1.0 / (row_devices * n * total_diags) ** 0.5,
    )
    return pair_out, rows, cols, kgrad.reshape(3, 3, ch, ch), bgrad.reshape(ch)


def solution(mesh):
    in_specs = (
        P(None, ("grp", "row")),
        P(None, ("grp", "row")),
        P(),
        P(),
        P(None, ("grp", "row"), "diag"),
        P(("grp", "row")),
        P("grp"),
        P("grp"),
    )
    out_specs = (
        P(None, ("grp", "row"), "diag"),
        P(None, ("grp", "row")),
        P(None, ("grp", "row")),
        P("grp", None, None, None),
        P("grp"),
    )
    return jax.shard_map(local, mesh=mesh, in_specs=in_specs, out_specs=out_specs, check_vma=False)
```

time: 58.1 us -> 49.7 us (0.86)
  waiting for transfers between devices: 10.6 us -> 4.13 us
  local copies, waits for them, and re-layouts: 3.15 us -> 0.02 us
  Pallas kernels: 27.2 us -> 28.9 us
  starting transfers between devices: 6.83 us -> 5.22 us
  blocking collectives: 6.72 us -> 8.21 us
    ppermute x4, waiting for transfers between devices: 10.6 us -> 4.13 us  [swapped(): lax.ppermute(value, axis, [(i, i ^ bit) for i in range(lax.axis_size(axis...]
    pallas_call x1 -> x5, Pallas kernels: 27.2 us -> 28.9 us  [the longest x1 17.7 us: tile_call(): pl.pallas_call(tile_kernel, out_shape=(jax.ShapeDtypeStruct((blocks * ch,...]
    ppermute x4, starting transfers between devices: 6.83 us -> 5.22 us  [swapped(): lax.ppermute(value, axis, [(i, i ^ bit) for i in range(lax.axis_size(axis...]
    all_gather x1, blocking collectives: 6.72 us -> 8.21 us  [local(): gathered = lax.all_gather(bins, 'row')]
    mul x3 -> x0, other arithmetic: 1.15 us -> none  [the longest x1 0.62 us: local(): both[ch:2 * ch] * embed_scale]
    dynamic_slice x1 -> x0, local copies, waits for them, and re-layouts: 0.85 us -> none  [local(): sent = lax.dynamic_index_in_dim(halves, 1 - mine, 0, False)]
    add x4, other arithmetic: 0.04 us -> 0.84 us  [local(): sums, whole = (kept + came[:own], sent[own:] + came[own:])]
    mul x1 -> x0, local copies, waits for them, and re-layouts: 0.77 us -> none  [local(): kernel_grad * weight_scale]
  transfers between devices with their start and end apart: 4 -> 4, of which waited for: 4 -> 2; matrix products, arithmetic and copies ran while one was open for 0% -> 0% of each run, Pallas kernels for 0% -> 18%
where the time goes in v2:
time: 49.7 us; the launch traced here: 49.4 us
  Pallas kernels  28.9 us (58%)
  blocking collectives  8.21 us (17%)
  starting transfers between devices  5.22 us (11%)
  waiting for transfers between devices  4.13 us (8%)
  between operations  2.01 us (4%)
  other arithmetic  0.86 us (2%)
    pallas_call x1, Pallas kernels, tile_call(): pl.pallas_call(tile_kernel, out_shape=(jax.ShapeDtypeStruct((blocks * ch,...  17.7 us
    pallas_call x2, Pallas kernels, out_call(): pl.pallas_call(body, out_shape=jax.ShapeDtypeStruct((ch, n, n), jnp.bfloa...  8.73 us
    all_gather x1, blocking collectives, local(): gathered = lax.all_gather(bins, 'row')  8.21 us
    ppermute x4, starting transfers between devices, swapped(): lax.ppermute(value, axis, [(i, i ^ bit) for i in range(lax.axis_size(axis...  5.22 us
    ppermute x4, waiting for transfers between devices, swapped(): lax.ppermute(value, axis, [(i, i ^ bit) for i in range(lax.axis_size(axis...  4.13 us
    pallas_call x1, Pallas kernels, pack_call(): pl.pallas_call(pack_kernel, out_shape=(jax.ShapeDtypeStruct((2 * ch + 16,...  1.76 us
  transfers between devices with their start and end apart: 4, of which 2 were waited for; matrix products, arithmetic and copies ran while one was open for 0% of the time, Pallas kernels for 18%

profile of v2, /device:TPU:0, one launch (start us, length us, event | category | flops | bytes accessed | tf_op | source)
XLA Modules:
  0.0 49.4 jit_solution(7149211335764286802)
XLA Ops:
  1.9 1.8 %pack.1 = (bf16[80,128]{1,0:T(8,128)(2,1)}, bf16[4,32,288]{2,1,0:T(8,128)(2,1)}) custom-call(bf16[32,128]{1,0:T(8,128)(2,1)} %emb_cols.1, bf16[32,128]{1,0:T(8,128)(2,1)} %emb_rows.1, s32[1,128]{1,0:T(1,128)} %bitcast.21, s32[1,1]{1,0:T(1,128)} %bitcast.12.dil, s32[1,1]{1,0:T(1,128)} %bitcast.15.band, bf16[3,3,32,32]{3,2,1,0:T(8,128)(2,1)} %kernel.1), custom_call_target="tpu_custom_call" | custom-call | tf_op jit(solution)/shard_map/pack/pallas_call | solution.py:54
  3.7 8.2 %all-gather = bf16[320,128]{1,0:T(8,128)(2,1)} all-gather(bf16[80,128]{1,0:T(8,128)(2,1)} %get-tuple-element.19), channel_id=2, replica_groups=mesh['grp'=2,'row'=4,'diag'=4] {'row'}, dimensions={0}, use_global_device_ids=true | all-gather | bytes 102400 | tf_op jit(solution)/shard_map/all_gather | solution.py:715
  11.9 17.7 %tile.1 = (f32[128,128]{1,0:T(8,128)}, f32[224,128]{1,0:T(8,128)}, bf16[144,96,128]{2,1,0:T(8,128)(2,1)}, f32[144,40,128]{2,1,0:T(8,128)}) custom-call(bf16[4,80,128]{2,1,0:T(8,128)(2,1)} %bitcast.18, bf16[4,32,288]{2,1,0:T(8,128)(2,1)} %get-tuple-element.20.weights.refs_0_, bf16[32,128,128]{2,1,0:T(8,128)(2,1)} %cot_hbm.1), custom_call_target="tpu_custom_call" | custom-call | flops 905969664 | bytes 8388608 | tf_op jit(solution)/shard_map/tile/pallas_call | solution.py:627
  29.6 0.8 %collective-permute-start = (f32[224,128]{1,0:T(8,128)}, f32[224,128]{1,0:T(8,128)S(1)}, u32[]{:S(2)}, u32[]{:S(2)}) collective-permute-start(f32[224,128]{1,0:T(8,128)} %get-tuple-element.22), channel_id=1, source_target_pairs={{0,8},{4,12},{8,0},{12,4},{1,9},{5,13},{9,1},{13,5},{2,10},{6,14},... | collective-permute-start | bytes 344072 | tf_op jit(solution)/shard_map/ppermute | solution.py:705
  30.4 0.0 copy-start
  30.4 5.1 %outputs.2.refs_5_ = bf16[32,128,128]{2,1,0:T(8,128)(2,1)} custom-call(bf16[4,32,288]{2,1,0:T(8,128)(2,1)} %get-tuple-element.20.weights.refs_0_, f32[1,32]{1,0:T(1,128)} %bitcast.19, s32[1,1]{1,0:T(1,128)} %bitcast.13.refs_2_, bf16[144,96,128]{2,1,0:T(8,128)(2,1)} %get-tuple-element.23.refs_3_, f32[144,40,128]{2,1,0:T(8,128)} %get-tuple-element.24.refs_4_), custom_call_target="tpu_custom_call" | custom-call | flops 188743680 | bytes 4096000 | tf_op jit(solution)/shard_map/outputs/pallas_call | solution.py:591
  35.5 0.0 collective-permute-done
  35.5 0.8 %slice_add_fusion.2 = f32[96,128]{1,0:T(8,128)S(1)} fusion(f32[224,128]{1,0:T(8,128)S(1)} %collective-permute-done, f32[224,128]{1,0:T(8,128)} %get-tuple-element.22), kind=kLoop, calls=%fused_computation.4 | loop fusion | flops 12288 | bytes 147456 | tf_op jit(solution)/shard_map/add | solution.py:729
  36.3 0.0 copy-done
  36.3 0.1 collective-permute-start.1
  36.5 1.2 %collective-permute-done.1 = f32[160,128]{1,0:T(8,128)S(1)} collective-permute-done((f32[160,128]{1,0:T(8,128)S(1)}, f32[160,128]{1,0:T(8,128)S(1)}, u32[]{:S(2)}, u32[]{:S(2)}) %collective-permute-start.1) | collective-permute-done | bytes 81952 | tf_op jit(solution)/shard_map/ppermute | solution.py:705
  37.7 1.6 %collective-permute-start.2 = (f32[160,128]{1,0:T(8,128)S(1)}, f32[160,128]{1,0:T(8,128)S(1)}, u32[]{:S(2)}, u32[]{:S(2)}) collective-permute-start(f32[160,128]{1,0:T(8,128)S(1)} %pad_maximum_fusion.1), channel_id=1, source_target_pairs={{0,1},{1,0},{2,3},{3,2},{4,5},{5,4},{6,7},{7,6},{8,9},{9,8},{10,11... | collective-permute-start | bytes 245768 | tf_op jit(solution)/shard_map/ppermute | solution.py:705
  39.4 2.9 %collective-permute-done.2 = f32[160,128]{1,0:T(8,128)S(1)} collective-permute-done((f32[160,128]{1,0:T(8,128)S(1)}, f32[160,128]{1,0:T(8,128)S(1)}, u32[]{:S(2)}, u32[]{:S(2)}) %collective-permute-start.2) | collective-permute-done | bytes 81952 | tf_op jit(solution)/shard_map/ppermute | solution.py:705
  42.3 2.7 %collective-permute-start.3 = (f32[160,128]{1,0:T(8,128)S(1)}, f32[160,128]{1,0:T(8,128)S(1)}, u32[]{:S(2)}, u32[]{:S(2)}) collective-permute-start(f32[160,128]{1,0:T(8,128)S(1)} %fusion.refs_0_), channel_id=1, source_target_pairs={{0,2},{1,3},{2,0},{3,1},{4,6},{5,7},{6,4},{7,5},{8,10},{9,11},{10,... | collective-permute-start | bytes 245768 | tf_op jit(solution)/shard_map/ppermute | solution.py:705
  45.0 3.7 %outputs.3 = bf16[32,128,128]{2,1,0:T(8,128)(2,1)} custom-call(bf16[4,32,288]{2,1,0:T(8,128)(2,1)} %get-tuple-element.20.weights.refs_0_, f32[1,32]{1,0:T(1,128)} %bitcast.20, s32[1,1]{1,0:T(1,128)} %bitcast.14.refs_2_, bf16[144,96,128]{2,1,0:T(8,128)(2,1)} %get-tuple-element.23.refs_3_, ...), custom_call_target="tpu_custom_call", output_to_operand_aliasing={{}: (5, {})} | custom-call | flops 113246208 | bytes 2457600 | tf_op jit(solution)/shard_map/outputs/pallas_call | solution.py:591
  48.6 0.0 collective-permute-done.3.refs_1_
  48.6 0.8 %finish.1 = (f32[32,128]{1,0:T(8,128)}, f32[32,128]{1,0:T(8,128)}, f32[9,32,32]{2,1,0:T(8,128)}, f32[1,32]{1,0:T(1,128)}) custom-call(f32[160,128]{1,0:T(8,128)S(1)} %fusion.refs_0_, f32[160,128]{1,0:T(8,128)S(1)} %collective-permute-done.3.refs_1_), custom_call_target="tpu_custom_call" | custom-call | tf_op jit(solution)/shard_map/finish/pallas_call | solution.py:689
  (7 shorter events, 0.1 us)
Async XLA Ops:
  29.6 5.9 %collective-permute-start = (f32[224,128]{1,0:T(8,128)}, f32[224,128]{1,0:T(8,128)S(1)}, u32[]{:S(2)}, u32[]{:S(2)}) collective-permute-start(f32[224,128]{1,0:T(8,128)} %get-tuple-element.22), channel_id=1, source_target_pairs={{0,8},{4,12},{8,0},{12,4},{1,9},{5,13},{9,1},{13,5},{2,10},{6,14},... | collective-permute-start | bytes 344072 | tf_op jit(solution)/shard_map/ppermute | solution.py:705
  30.4 5.9 %copy-start = (f32[128,128]{1,0:T(8,128)S(1)}, f32[128,128]{1,0:T(8,128)}, u32[]{:S(2)}) copy-start(f32[128,128]{1,0:T(8,128)} %get-tuple-element.21) | copy-start | bytes 196612
  36.3 1.3 %collective-permute-start.1 = (f32[160,128]{1,0:T(8,128)S(1)}, f32[160,128]{1,0:T(8,128)S(1)}, u32[]{:S(2)}, u32[]{:S(2)}) collective-permute-start(f32[160,128]{1,0:T(8,128)S(1)} %pad_maximum_fusion), channel_id=1, source_target_pairs={{0,4},{4,0},{8,12},{12,8},{1,5},{5,1},{9,13},{13,9},{2,6},{6,2},{1... | collective-permute-start | bytes 245768 | tf_op jit(solution)/shard_map/ppermute | solution.py:705
  37.7 4.6 %collective-permute-start.2 = (f32[160,128]{1,0:T(8,128)S(1)}, f32[160,128]{1,0:T(8,128)S(1)}, u32[]{:S(2)}, u32[]{:S(2)}) collective-permute-start(f32[160,128]{1,0:T(8,128)S(1)} %pad_maximum_fusion.1), channel_id=1, source_target_pairs={{0,1},{1,0},{2,3},{3,2},{4,5},{5,4},{6,7},{7,6},{8,9},{9,8},{10,11... | collective-permute-start | bytes 245768 | tf_op jit(solution)/shard_map/ppermute | solution.py:705
  42.3 6.3 %collective-permute-start.3 = (f32[160,128]{1,0:T(8,128)S(1)}, f32[160,128]{1,0:T(8,128)S(1)}, u32[]{:S(2)}, u32[]{:S(2)}) collective-permute-start(f32[160,128]{1,0:T(8,128)S(1)} %fusion.refs_0_), channel_id=1, source_target_pairs={{0,2},{1,3},{2,0},{3,1},{4,6},{5,7},{6,4},{7,5},{8,10},{9,11},{10,... | collective-permute-start | bytes 245768 | tf_op jit(solution)/shard_map/ppermute | solution.py:705

commit v3 on v2

--- a/solution.py
+++ b/solution.py
@@ -6,12 +6,13 @@
 from jax.sharding import PartitionSpec as P
 
 MAXDIL = 4
+BACK = 64
 EDGE = 2 * MAXDIL
 SLOT = 2 * EDGE
 GELU_C = 0.7978845608028654
 GELU_A = 0.044715
 WORD_BITS = 6
-VMEM_LIMIT = (65472 - 900) * 1024
+VMEM_LIMIT = 54600 * 1024
 OUT_LIMIT = (65472 - 1500) * 1024
 
 
@@ -55,7 +56,7 @@
         pack_kernel,
         out_shape=(
             jax.ShapeDtypeStruct((2 * ch + 16, n), jnp.bfloat16),
-            jax.ShapeDtypeStruct((4, ch, 9 * ch), jnp.bfloat16),
+            jax.ShapeDtypeStruct((16, ch, 9 * ch), jnp.bfloat16),
         ),
         in_specs=[vmem] * 6,
         out_specs=(vmem, vmem),
@@ -67,13 +68,15 @@
 
 
 def tile_kernel(
-    gathered, weights, cot_hbm,
+    gathered, weights_hbm, cot_hbm,
     kept, sent, act_hbm, held_hbm,
     act, held, grd, slope, halo, edge, gedge, dfix, cols, colv, accs, kacc, kedge,
-    place, nears, cot, sems,
+    place, nears, spreads, cot, weights, sems,
 ):
     cot_in = pltpu.make_async_copy(cot_hbm, cot, sems.at[0])
     cot_in.start()
+    weights_in = pltpu.make_async_copy(weights_hbm.at[pl.ds(0, 4)], weights, sems.at[1])
+    weights_in.start()
     ch = cot.shape[0]
     n = cot.shape[1]
     sub = ch // 8
@@ -160,13 +163,13 @@
     whole = lax.broadcasted_iota(jnp.int32, (n, n), 0)
 
     def packs_step(g, carry):
-        for two in range(2):
-            p0 = 4 * g + 2 * two
+        for two in range(4):
+            p0 = 8 * g + 2 * two
             rows_at = [pack_lanes(lane1, p0 + w)[0][:1] for w in range(2)]
             to_row = jnp.concatenate(
                 [(whole == x).astype(f32).astype(bf16) for x in rows_at], axis=1
             )
-            place[2 * g + two] = to_row
+            place[4 * g + two] = to_row
             found = jnp.dot(own16, to_row, preferred_element_type=f32)
             for w in range(2):
                 p = p0 + w
@@ -181,16 +184,22 @@
                 halo[p] = a
         return carry
 
-    lax.fori_loop(0, SLOT // 4, packs_step, 0)
+    lax.fori_loop(0, SLOT // 8, packs_step, 0)
 
     for at in list(range(2 * extra)) + list(range(n + 2 * extra, n + 4 * extra)):
         grd[at] = jnp.zeros(grd.shape[1:], bf16)
 
+    for g in range(n // 16):
+        turned = pltpu.roll(own, (n - 16 * g) % n, 1).astype(bf16) if g else own16
+        wide = jnp.dot(turned[:, :16], ones, preferred_element_type=f32)
+        for u in range(16):
+            spreads[16 * g + u] = wide[: ch + 8, u * n : (u + 1) * n]
+
     def rows_step(g, carry):
-        base = pl.multiple_of(g * 16, 16)
-        turned = pltpu.roll(own, (n - base) & (n - 1), 1).astype(bf16)
-        for u, (rows, rows_v) in enumerate(spread16(turned)):
+        base = pl.multiple_of(g * 32, 32)
+        for u in range(32):
             i = base + u
+            rows, rows_v = spreads[i, :ch, :].reshape(sub, 8, n), spreads[i, ch:, :]
             here = lane8 >= i
             col = jnp.where(here[None], cols[1], cols[2])
             col_v = jnp.where(here, colv[1], colv[2])
@@ -201,7 +210,7 @@
             store_turns(act, i + extra, a, False)
         return carry
 
-    lax.fori_loop(0, n // 16, rows_step, 0)
+    lax.fori_loop(0, n // 32, rows_step, 0)
 
     def grads_step(g, carry):
         base = pl.multiple_of(g * 16, 16)
@@ -221,19 +230,21 @@
     cot_in.wait()
     lax.fori_loop(0, n // 16, grads_step, 0)
 
-    def edges_step(p, carry):
-        row = small(pack_lanes(lane16, p)[0])
-        a = x = jnp.zeros((2, 16, n), bf16)
-        for m in range(n // SLOT):
-            i = p + m * SLOT
-            here = (row == small(i))[None]
-            a = jnp.where(here, half(act[i + extra, ch : 2 * ch, :]), a)
-            x = jnp.where(here, half(grd[i + 2 * extra, ch : 2 * ch, :]), x)
-        edge[p] = a.reshape(ch, n)
-        gedge[p] = x.reshape(ch, n)
-        return carry
-
-    lax.fori_loop(0, SLOT, edges_step, 0)
+    def edges_step(g, carry):
+        for w in range(4):
+            p = 4 * g + w
+            row = small(pack_lanes(lane16, p)[0])
+            a = x = jnp.zeros((2, 16, n), bf16)
+            for m in range(n // SLOT):
+                i = p + m * SLOT
+                here = (row == small(i))[None]
+                a = jnp.where(here, half(act[i + extra, ch : 2 * ch, :]), a)
+                x = jnp.where(here, half(grd[i + 2 * extra, ch : 2 * ch, :]), x)
+            edge[p] = a.reshape(ch, n)
+            gedge[p] = x.reshape(ch, n)
+        return carry
+
+    lax.fori_loop(0, SLOT // 4, edges_step, 0)
 
     lane_tall = lax.broadcasted_iota(jnp.int32, (tall, n), 1)
     near = jnp.where(
@@ -275,6 +286,7 @@
     act_out = pltpu.make_async_copy(act, act_hbm, sems.at[3])
     act_out.start()
 
+    weights_in.wait()
     w_in = weights[1]
     w_out_edge, w_in_edge = weights[2, :, : 6 * ch], weights[3, :, : 6 * ch]
     crossing = crossings()
@@ -331,11 +343,11 @@
             dfix[p + w] = da[:, w * n : (w + 1) * n].reshape(sub, 8, n)
 
     def fix_step(g, carry):
-        fix_pair(4 * g)
-        fix_pair(4 * g + 2)
-        return carry
-
-    lax.fori_loop(0, SLOT // 4, fix_step, 0)
+        for w in range(4):
+            fix_pair(8 * g + 2 * w)
+        return carry
+
+    lax.fori_loop(0, SLOT // 8, fix_step, 0)
     fixes_out = pltpu.make_async_copy(
         held.at[pl.ds(n, SLOT)], held_hbm.at[pl.ds(n, SLOT)], sems.at[4]
     )
@@ -360,7 +372,7 @@
 
     kacc[...] = jnp.zeros(kacc.shape, f32)
     accs[...] = jnp.zeros(accs.shape, f32)
-    def spreads(i):
+    def back_rows(i):
         both = two_rows(grd, i + 2 * extra, -r)
         da = jnp.dot(w_in, both, preferred_element_type=f32)
         return [da[:, w * n : (w + 1) * n].reshape(sub, 8, n) for w in range(2)]
@@ -379,16 +391,16 @@
         )
 
     def back_step(g, carry):
-        base = pl.multiple_of(g * 16, 16)
+        base = pl.multiple_of(g * BACK, BACK)
         total = None
         racc, c0, c1, bacc = accs[1], accs[4], accs[5], accs[7]
-        for u in range(0, 16, 2):
+        for u in range(0, BACK, 2):
             i = base + u
             part = kernel_part(i)
             total = part if total is None else total + part
-            for w, da in enumerate(spreads(i)):
+            for w, da in enumerate(back_rows(i)):
                 slot = ((lane8 - (i + w) + EDGE) & (n - 1)) < SLOT
-                da = da - jnp.where(slot[None], dfix[u + w], 0.0)
+                da = da - jnp.where(slot[None], dfix[(u + w) % SLOT], 0.0)
                 gg = grd[i + w + 2 * extra, ch : 2 * ch, :].astype(f32).reshape(sub, 8, n)
                 bacc = bacc + gg
                 dx = gg + slope[i + w + extra] * da
@@ -402,17 +414,16 @@
         kacc[...] += total
         return carry
 
-    lax.fori_loop(0, n // 16, back_step, 0)
+    lax.fori_loop(0, n // BACK, back_step, 0)
 
     def add_columns(dx, t):
         for b in range(4):
             accs[3 + b] += jnp.where((t == b - 1)[None], dx, 0.0)
 
-    def near_sums(g, carry):
-        y0 = 2 * g
+    def near_sums(y0):
         i0 = near_row(y0)
         which = jnp.where(y0 < extra, 0, 2)
-        for w, da in enumerate(spreads(i0)):
+        for w, da in enumerate(back_rows(i0)):
             i = i0 + w
             e, d = near_lanes(i)
             fix = dfix[SLOT + y0 + w]
@@ -422,16 +433,19 @@
             add_columns(outer, (i + d) >> 7)
             total = jnp.sum(inner + outer, axis=2, keepdims=True)
             accs[which] += jnp.where((lane8 == (i & (n - 1)))[None], total, 0.0)
-        kacc[...] += kernel_part(i0)
-        return carry
-
-    lax.fori_loop(0, extra, near_sums, 0)
+        return kernel_part(i0)
+
+    def near_pair(g, carry):
+        kacc[...] += near_sums(4 * g) + near_sums(4 * g + 2)
+        return carry
+
+    lax.fori_loop(0, extra // 2, near_pair, 0)
 
     def pack_sums(g, carry):
-        for two in range(2):
+        for two in range(4):
             dxs = []
             for w in range(2):
-                p = 4 * g + 2 * two + w
+                p = 8 * g + 2 * two + w
                 row, e = pack_lanes(lane8, p)
                 dx = slope[packs + p] * dfix[p]
                 add_columns(dx, (row + jnp.where(e < 0, e, e + n)) >> 7)
@@ -443,14 +457,14 @@
                 rest = rest - part.astype(f32)
                 parts.append(part)
             found = lax.dot_general(
-                jnp.concatenate(parts, axis=0), place[2 * g + two],
+                jnp.concatenate(parts, axis=0), place[4 * g + two],
                 (((1,), (1,)), ((), ())), preferred_element_type=f32,
             )
             total = found[:ch] + found[ch : 2 * ch] + found[2 * ch :]
             accs[1] += total.reshape(sub, 8, n)
         return carry
 
-    lax.fori_loop(0, SLOT // 4, pack_sums, 0)
+    lax.fori_loop(0, SLOT // 8, pack_sums, 0)
 
     half_blocks = blocks // 2
     mine = r_id // half_blocks
@@ -632,7 +646,7 @@
             jax.ShapeDtypeStruct((n + SLOT, 3 * ch, n), bf16),
             jax.ShapeDtypeStruct((n + SLOT, ch + 8, n), f32),
         ),
-        in_specs=[vmem, vmem, hbm],
+        in_specs=[vmem, hbm, hbm],
         out_specs=(vmem, vmem, hbm, hbm),
         scratch_shapes=[
             pltpu.VMEM((n + SLOT, 3 * ch, n), bf16),
@@ -650,7 +664,9 @@
             pltpu.VMEM((6 * ch, ch), f32),
             pltpu.VMEM((SLOT // 2, n, 2 * n), bf16),
             pltpu.VMEM((near, sub + 1, 8, n), f32),
+            pltpu.VMEM((n, ch + 8, n), f32),
             pltpu.VMEM((ch, n, n), bf16),
+            pltpu.VMEM((4, ch, 9 * ch), bf16),
             pltpu.SemaphoreType.DMA((5,)),
         ],
         compiler_params=pltpu.CompilerParams(vmem_limit_bytes=VMEM_LIMIT),

time: 49.7 us -> 43 us (0.87)
  Pallas kernels: 28.9 us -> 23.5 us
  blocking collectives: 8.21 us -> 6.51 us
  starting transfers between devices: 5.22 us -> 6.46 us
  other arithmetic: 0.86 us -> 0.06 us
    pallas_call x1, Pallas kernels: 17.7 us -> 12.2 us  [tile_call(): pl.pallas_call(tile_kernel, out_shape=(jax.ShapeDtypeStruct((blocks * ch,...]
    all_gather x1, blocking collectives: 8.21 us -> 6.51 us  [local(): gathered = lax.all_gather(bins, 'row')]
    ppermute x4, starting transfers between devices: 5.22 us -> 6.46 us  [swapped(): lax.ppermute(value, axis, [(i, i ^ bit) for i in range(lax.axis_size(axis...]
    add x4, other arithmetic: 0.84 us -> 0.03 us  [local(): sums, whole = (kept + came[:own], sent[own:] + came[own:])]
  transfers between devices with their start and end apart: 4 -> 4, of which waited for: 2 -> 2; matrix products, arithmetic and copies ran while one was open for 0% -> 0% of each run, Pallas kernels for 18% -> 20%
where the time goes in v3:
time: 43 us; the launch traced here: 42.7 us
  Pallas kernels  23.5 us (55%)
  blocking collectives  6.51 us (15%)
  starting transfers between devices  6.46 us (15%)
  waiting for transfers between devices  4.14 us (10%)
  between operations  2.02 us (5%)
    pallas_call x1, Pallas kernels, tile_call(): pl.pallas_call(tile_kernel, out_shape=(jax.ShapeDtypeStruct((blocks * ch,...  12.2 us
    pallas_call x2, Pallas kernels, out_call(): pl.pallas_call(body, out_shape=jax.ShapeDtypeStruct((ch, n, n), jnp.bfloa...  8.71 us
    all_gather x1, blocking collectives, local(): gathered = lax.all_gather(bins, 'row')  6.51 us
    ppermute x4, starting transfers between devices, swapped(): lax.ppermute(value, axis, [(i, i ^ bit) for i in range(lax.axis_size(axis...  6.46 us
    ppermute x4, waiting for transfers between devices, swapped(): lax.ppermute(value, axis, [(i, i ^ bit) for i in range(lax.axis_size(axis...  4.14 us
    pallas_call x1, Pallas kernels, pack_call(): pl.pallas_call(pack_kernel, out_shape=(jax.ShapeDtypeStruct((2 * ch + 16,...  1.89 us
  transfers between devices with their start and end apart: 4, of which 2 were waited for; matrix products, arithmetic and copies ran while one was open for 0% of the time, Pallas kernels for 20%

profile of v3, /device:TPU:0, one launch (start us, length us, event | category | flops | bytes accessed | tf_op | source)
XLA Modules:
  0.0 42.7 jit_solution(18376920419231008293)
XLA Ops:
  1.9 1.9 %pack.1 = (bf16[80,128]{1,0:T(8,128)(2,1)}, bf16[16,32,288]{2,1,0:T(8,128)(2,1)}) custom-call(bf16[32,128]{1,0:T(8,128)(2,1)} %emb_cols.1, bf16[32,128]{1,0:T(8,128)(2,1)} %emb_rows.1, s32[1,128]{1,0:T(1,128)} %bitcast.21, s32[1,1]{1,0:T(1,128)} %bitcast.12.dil, s32[1,1]{1,0:T(1,128)} %bitcast.15.band, bf16[3,3,32,32]{3,2,1,0:T(8,128)(2,1)} %kernel.1), custom_call_target="tpu_custom_call" | custom-call | tf_op jit(solution)/shard_map/pack/pallas_call | solution.py:55
  3.8 6.5 %all-gather = bf16[320,128]{1,0:T(8,128)(2,1)S(1)} all-gather(bf16[80,128]{1,0:T(8,128)(2,1)} %get-tuple-element.19), channel_id=2, replica_groups=mesh['grp'=2,'row'=4,'diag'=4] {'row'}, dimensions={0}, use_global_device_ids=true | all-gather | bytes 102400 | tf_op jit(solution)/shard_map/all_gather | solution.py:731
  10.3 12.2 %tile.1 = (f32[128,128]{1,0:T(8,128)S(1)}, f32[224,128]{1,0:T(8,128)S(1)}, bf16[144,96,128]{2,1,0:T(8,128)(2,1)}, f32[144,40,128]{2,1,0:T(8,128)}) custom-call(bf16[4,80,128]{2,1,0:T(8,128)(2,1)S(1)} %bitcast.16, bf16[16,32,288]{2,1,0:T(8,128)(2,1)} %get-tuple-element.20.weights_hbm.refs_0_, bf16[32,128,128]{2,1,0:T(8,128)(2,1)} %cot_hbm.1), custom_call_target="tpu_custom_call" | custom-call | flops 905969664 | bytes 8388608 | tf_op jit(solution)/shard_map/tile/pallas_call | solution.py:641
  22.5 2.0 %collective-permute-start = (f32[224,128]{1,0:T(8,128)S(1)}, f32[224,128]{1,0:T(8,128)S(1)}, u32[]{:S(2)}, u32[]{:S(2)}) collective-permute-start(f32[224,128]{1,0:T(8,128)S(1)} %get-tuple-element.22), channel_id=1, source_target_pairs={{0,8},{4,12},{8,0},{12,4},{1,9},{5,13},{9,1},{13,5},{2,10},{6,14},... | collective-permute-start | bytes 344072 | tf_op jit(solution)/shard_map/ppermute | solution.py:721
  24.5 5.1 %outputs.2.refs_5_ = bf16[32,128,128]{2,1,0:T(8,128)(2,1)} custom-call(bf16[16,32,288]{2,1,0:T(8,128)(2,1)} %get-tuple-element.20.weights_hbm.refs_0_, f32[1,32]{1,0:T(1,128)} %bitcast.19, s32[1,1]{1,0:T(1,128)} %bitcast.13.refs_2_, bf16[144,96,128]{2,1,0:T(8,128)(2,1)} %get-tuple-element.23.refs_3_, f32[144,40,128]{2,1,0:T(8,128)} %get-tuple-element.24.refs_4_), custom_call_target="tpu_custom_call" | custom-call | flops 188743680 | bytes 4096000 | tf_op jit(solution)/shard_map/outputs/pallas_call | solution.py:605
  29.6 0.0 collective-permute-done
  29.7 0.1 collective-permute-start.1
  29.8 1.2 %collective-permute-done.1 = f32[160,128]{1,0:T(8,128)S(1)} collective-permute-done((f32[160,128]{1,0:T(8,128)S(1)}, f32[160,128]{1,0:T(8,128)S(1)}, u32[]{:S(2)}, u32[]{:S(2)}) %collective-permute-start.1) | collective-permute-done | bytes 81952 | tf_op jit(solution)/shard_map/ppermute | solution.py:721
  31.1 1.6 %collective-permute-start.2 = (f32[160,128]{1,0:T(8,128)S(1)}, f32[160,128]{1,0:T(8,128)S(1)}, u32[]{:S(2)}, u32[]{:S(2)}) collective-permute-start(f32[160,128]{1,0:T(8,128)S(1)} %pad_maximum_fusion.1), channel_id=1, source_target_pairs={{0,1},{1,0},{2,3},{3,2},{4,5},{5,4},{6,7},{7,6},{8,9},{9,8},{10,11... | collective-permute-start | bytes 245768 | tf_op jit(solution)/shard_map/ppermute | solution.py:721
  32.7 2.9 %collective-permute-done.2 = f32[160,128]{1,0:T(8,128)S(1)} collective-permute-done((f32[160,128]{1,0:T(8,128)S(1)}, f32[160,128]{1,0:T(8,128)S(1)}, u32[]{:S(2)}, u32[]{:S(2)}) %collective-permute-start.2) | collective-permute-done | bytes 81952 | tf_op jit(solution)/shard_map/ppermute | solution.py:721
  35.6 2.7 %collective-permute-start.3 = (f32[160,128]{1,0:T(8,128)S(1)}, f32[160,128]{1,0:T(8,128)S(1)}, u32[]{:S(2)}, u32[]{:S(2)}) collective-permute-start(f32[160,128]{1,0:T(8,128)S(1)} %fusion.refs_0_), channel_id=1, source_target_pairs={{0,2},{1,3},{2,0},{3,1},{4,6},{5,7},{6,4},{7,5},{8,10},{9,11},{10,... | collective-permute-start | bytes 245768 | tf_op jit(solution)/shard_map/ppermute | solution.py:721
  38.3 3.7 %outputs.3 = bf16[32,128,128]{2,1,0:T(8,128)(2,1)} custom-call(bf16[16,32,288]{2,1,0:T(8,128)(2,1)} %get-tuple-element.20.weights_hbm.refs_0_, f32[1,32]{1,0:T(1,128)} %bitcast.20, s32[1,1]{1,0:T(1,128)} %bitcast.14.refs_2_, bf16[144,96,128]{2,1,0:T(8,128)(2,1)} %get-tuple-element.23.refs_3_, ...), custom_call_target="tpu_custom_call", output_to_operand_aliasing={{}: (5, {})} | custom-call | flops 113246208 | bytes 2457600 | tf_op jit(solution)/shard_map/outputs/pallas_call | solution.py:605
  42.0 0.0 collective-permute-done.3.refs_1_
  42.0 0.8 %finish.1 = (f32[32,128]{1,0:T(8,128)}, f32[32,128]{1,0:T(8,128)}, f32[9,32,32]{2,1,0:T(8,128)}, f32[1,32]{1,0:T(1,128)}) custom-call(f32[160,128]{1,0:T(8,128)S(1)} %fusion.refs_0_, f32[160,128]{1,0:T(8,128)S(1)} %collective-permute-done.3.refs_1_), custom_call_target="tpu_custom_call" | custom-call | tf_op jit(solution)/shard_map/finish/pallas_call | solution.py:705
  (8 shorter events, 0.1 us)
Async XLA Ops:
  22.5 7.1 %collective-permute-start = (f32[224,128]{1,0:T(8,128)S(1)}, f32[224,128]{1,0:T(8,128)S(1)}, u32[]{:S(2)}, u32[]{:S(2)}) collective-permute-start(f32[224,128]{1,0:T(8,128)S(1)} %get-tuple-element.22), channel_id=1, source_target_pairs={{0,8},{4,12},{8,0},{12,4},{1,9},{5,13},{9,1},{13,5},{2,10},{6,14},... | collective-permute-start | bytes 344072 | tf_op jit(solution)/shard_map/ppermute | solution.py:721
  29.7 1.3 %collective-permute-start.1 = (f32[160,128]{1,0:T(8,128)S(1)}, f32[160,128]{1,0:T(8,128)S(1)}, u32[]{:S(2)}, u32[]{:S(2)}) collective-permute-start(f32[160,128]{1,0:T(8,128)S(1)} %pad_maximum_fusion), channel_id=1, source_target_pairs={{0,4},{4,0},{8,12},{12,8},{1,5},{5,1},{9,13},{13,9},{2,6},{6,2},{1... | collective-permute-start | bytes 245768 | tf_op jit(solution)/shard_map/ppermute | solution.py:721
  31.1 4.6 %collective-permute-start.2 = (f32[160,128]{1,0:T(8,128)S(1)}, f32[160,128]{1,0:T(8,128)S(1)}, u32[]{:S(2)}, u32[]{:S(2)}) collective-permute-start(f32[160,128]{1,0:T(8,128)S(1)} %pad_maximum_fusion.1), channel_id=1, source_target_pairs={{0,1},{1,0},{2,3},{3,2},{4,5},{5,4},{6,7},{7,6},{8,9},{9,8},{10,11... | collective-permute-start | bytes 245768 | tf_op jit(solution)/shard_map/ppermute | solution.py:721
  35.6 6.3 %collective-permute-start.3 = (f32[160,128]{1,0:T(8,128)S(1)}, f32[160,128]{1,0:T(8,128)S(1)}, u32[]{:S(2)}, u32[]{:S(2)}) collective-permute-start(f32[160,128]{1,0:T(8,128)S(1)} %fusion.refs_0_), channel_id=1, source_target_pairs={{0,2},{1,3},{2,0},{3,1},{4,6},{5,7},{6,4},{7,5},{8,10},{9,11},{10,... | collective-permute-start | bytes 245768 | tf_op jit(solution)/shard_map/ppermute | solution.py:721

commit v4 on v3

--- a/solution.py
+++ b/solution.py
@@ -1,3 +1,5 @@
+import functools
+
 import jax
 import jax.numpy as jnp
 from jax import lax
@@ -29,7 +31,7 @@
     return [(ta, tb) for ta in range(3) for tb in range(3) if ta != tb]
 
 
-def pack_kernel(emb_cols, emb_rows, valid, dil, band, kernel, bins, weights):
+def pack_kernel(emb_cols, emb_rows, valid, dil, band, kernel, bias, bins, weights):
     f32, bf16 = jnp.float32, jnp.bfloat16
     ch, n = emb_cols.shape
     bins[:ch] = emb_cols[...]
@@ -47,9 +49,21 @@
     weights[1] = jnp.concatenate(turned, axis=1)
     weights[2, :, : 6 * ch] = jnp.concatenate([taps[t] for t in cross], axis=1)
     weights[3, :, : 6 * ch] = jnp.concatenate([turned[t] for t in cross], axis=1)
-
-
-def pack_call(emb_cols, emb_rows, valid, dil, band, kernel):
+    square = [lax.broadcasted_iota(jnp.int32, (ch, ch), x) for x in range(2)]
+    rest = jnp.sum(
+        jnp.where(square[0] == square[1], jnp.broadcast_to(bias[...], (ch, ch)), 0.0),
+        axis=1, keepdims=True,
+    )
+    lane = lax.broadcasted_iota(jnp.int32, (ch, 9 * ch), 1)
+    whole = jnp.zeros((ch, 9 * ch), f32)
+    for j in range(3):
+        part = rest.astype(bf16).astype(f32)
+        rest = rest - part
+        whole = jnp.where(lane == j, part, whole)
+    weights[4] = whole.astype(bf16)
+
+
+def pack_call(emb_cols, emb_rows, valid, dil, band, kernel, bias):
     ch, n = emb_cols.shape
     vmem = pl.BlockSpec(memory_space=pltpu.VMEM)
     return pl.pallas_call(
@@ -58,24 +72,25 @@
             jax.ShapeDtypeStruct((2 * ch + 16, n), jnp.bfloat16),
             jax.ShapeDtypeStruct((16, ch, 9 * ch), jnp.bfloat16),
         ),
-        in_specs=[vmem] * 6,
+        in_specs=[vmem] * 7,
         out_specs=(vmem, vmem),
         compiler_params=pltpu.CompilerParams(vmem_limit_bytes=65472 * 1024),
         name="pack",
     )(
-        emb_cols, emb_rows, valid.reshape(1, n), dil.reshape(1, 1), band.reshape(1, 1), kernel
+        emb_cols, emb_rows, valid.reshape(1, n), dil.reshape(1, 1), band.reshape(1, 1), kernel,
+        bias.reshape(1, ch),
     )
 
 
 def tile_kernel(
-    gathered, weights_hbm, cot_hbm,
-    kept, sent, act_hbm, held_hbm,
+    here, gathered, weights_hbm, cot_hbm,
+    kept, sent, act_hbm, held_hbm, pair_out,
     act, held, grd, slope, halo, edge, gedge, dfix, cols, colv, accs, kacc, kedge,
-    place, nears, spreads, cot, weights, sems,
+    place, nears, spreads, cot, weights, done, sems, done_sems,
 ):
     cot_in = pltpu.make_async_copy(cot_hbm, cot, sems.at[0])
     cot_in.start()
-    weights_in = pltpu.make_async_copy(weights_hbm.at[pl.ds(0, 4)], weights, sems.at[1])
+    weights_in = pltpu.make_async_copy(weights_hbm.at[pl.ds(0, 5)], weights, sems.at[1])
     weights_in.start()
     ch = cot.shape[0]
     n = cot.shape[1]
@@ -223,9 +238,8 @@
             store_turns(grd, i + 2 * extra, x, True)
         return carry
 
-    held_out = pltpu.make_async_copy(
-        held.at[pl.ds(0, n)], held_hbm.at[pl.ds(0, n)], sems.at[2]
-    )
+    later = pl.ds(16 * here, n - 16 * here)
+    held_out = pltpu.make_async_copy(held.at[later], held_hbm.at[later], sems.at[2])
     held_out.start()
     cot_in.wait()
     lax.fori_loop(0, n // 16, grads_step, 0)
@@ -283,7 +297,8 @@
         return carry
 
     lax.fori_loop(0, extra // 2, near_step, 0)
-    act_out = pltpu.make_async_copy(act, act_hbm, sems.at[3])
+    later = pl.ds(16 * here, n + SLOT - 16 * here)
+    act_out = pltpu.make_async_copy(act.at[later], act_hbm.at[later], sems.at[3])
     act_out.start()
 
     weights_in.wait()
@@ -353,6 +368,18 @@
     )
     fixes_out.start()
 
+    shift_by = bias_lanes(weights[4], n)
+    for g in range(here):
+        done[g] = output_rows(16 * g, 16 * g, n, act, held, weights[0], shift_by, r)
+    done_out = [
+        pltpu.make_async_copy(
+            done.at[g], pair_out.at[:, pl.ds(16 * g, 16), :], done_sems.at[g]
+        )
+        for g in range(here)
+    ]
+    for copy in done_out:
+        copy.start()
+
     for y in range(2 * extra):
         i = y - extra if y < extra else n + y - extra
         ta = 0 if y < extra else 2
@@ -509,6 +536,8 @@
     held_out.wait()
     act_out.wait()
     fixes_out.wait()
+    for copy in done_out:
+        copy.wait()
 
 
 def rows_of(ref, at, step):
@@ -519,13 +548,36 @@
     return jnp.concatenate([rows_of(ref, at, step), rows_of(ref, at + 1, step)], axis=1)
 
 
+def bias_lanes(parts, n):
+    ch = parts.shape[0]
+    parts = parts.astype(jnp.float32)
+    column = parts[:, :1] + parts[:, 1:2] + parts[:, 2:3]
+    return jnp.broadcast_to(column, (ch, n)).reshape(ch // 8, 8, n)
+
+
+def output_rows(i, k, fixes, act, held, w_out, shift_by, r):
+    ch, n = w_out.shape[0], act.shape[2]
+    lane8 = lax.broadcasted_iota(jnp.int32, (8, n), 1)
+    found = []
+    for u in range(0, 16, 2):
+        z = jnp.dot(
+            w_out, two_rows(act, k + u + MAXDIL, r), preferred_element_type=jnp.float32
+        )
+        for w in range(2):
+            slot = ((lane8 - (i + u + w) + EDGE) & (n - 1)) < SLOT
+            fix = held[fixes + u + w, :ch, :].reshape(ch // 8, 8, n)
+            y = (held[k + u + w, :ch, :] + z[:, w * n : (w + 1) * n]).reshape(ch // 8, 8, n)
+            y = y + shift_by + jnp.where(slot[None], fix, 0.0)
+            y = (y * held[k + u + w, ch:, :][None]).reshape(ch, n).astype(jnp.bfloat16)
+            found.append(pltpu.roll(y, (n - i - u - w) & (n - 1), 1))
+    return jnp.swapaxes(jnp.stack(found), 0, 1)
+
+
 def out_kernel(
-    start, count, weights_hbm, bias_hbm, dil_hbm, act_hbm, held_hbm, *refs
+    start, count, weights_hbm, dil_hbm, act_hbm, held_hbm, *refs
 ):
-    pair_out, weights, bias, act, held, done, dil, sems, act_sems, held_sems, done_sems = refs[-11:]
-    f32, bf16 = jnp.float32, jnp.bfloat16
+    pair_out, weights, act, held, done, dil, sems, act_sems, held_sems, done_sems = refs[-10:]
     ch, n = pair_out.shape[:2]
-    sub = ch // 8
 
     def part(hbm, vmem, sem, first, there):
         rows = pl.ds(pl.multiple_of(first, 16), 16)
@@ -545,7 +597,7 @@
     small = [
         pltpu.make_async_copy(a, b, sems.at[j])
         for j, (a, b) in enumerate(
-            ((dil_hbm, dil), (bias_hbm, bias), (weights_hbm.at[0], weights))
+            ((dil_hbm, dil), *((weights_hbm.at[4 * x], weights.at[x]) for x in range(2)))
         )
     ]
     for copy in small:
@@ -555,16 +607,10 @@
     for g in range(count):
         act_part(g + 1).start()
         held_part(g).start()
-    lane8 = lax.broadcasted_iota(jnp.int32, (8, n), 1)
     for copy in small:
         copy.wait()
-    w_out = weights[...]
-    square = [lax.broadcasted_iota(jnp.int32, (ch, ch), x) for x in range(2)]
-    shift_by = jnp.sum(
-        jnp.where(square[0] == square[1], jnp.broadcast_to(bias[...], (ch, ch)), 0.0),
-        axis=1, keepdims=True,
-    )
-    shift_by = jnp.broadcast_to(shift_by, (ch, n)).reshape(sub, 8, n)
+    w_out = weights[0]
+    shift_by = bias_lanes(weights[1], n)
     r = jnp.max(dil[...])
     fixes.wait()
     act_part(0).wait()
@@ -572,19 +618,9 @@
     def conv_step(g, carry):
         act_part(g + 1).wait()
         held_part(g).wait()
-        found = []
-        for u in range(0, 16, 2):
-            k = g * 16 + u
-            i = start * 16 + k
-            z = jnp.dot(w_out, two_rows(act, k + MAXDIL, r), preferred_element_type=f32)
-            for w in range(2):
-                slot = ((lane8 - (i + w) + EDGE) & (n - 1)) < SLOT
-                fix = held[count * 16 + u + w, :ch, :].reshape(sub, 8, n)
-                y = (held[k + w, :ch, :] + z[:, w * n : (w + 1) * n]).reshape(sub, 8, n)
-                y = y + shift_by + jnp.where(slot[None], fix, 0.0)
-                y = (y * held[k + w, ch:, :][None]).reshape(ch, n).astype(bf16)
-                found.append(pltpu.roll(y, (n - i - w) & (n - 1), 1))
-        done[g] = jnp.swapaxes(jnp.stack(found), 0, 1)
+        done[g] = output_rows(
+            (start + g) * 16, g * 16, count * 16, act, held, w_out, shift_by, r
+        )
         done_part(g).start()
         return carry
 
@@ -593,7 +629,7 @@
         done_part(g).wait()
 
 
-def out_call(start, count, made, weights, bias, dil, act, held):
+def out_call(start, count, made, weights, dil, act, held):
     _, ch3, n = act.shape
     ch = ch3 // 3
     hbm = pl.BlockSpec(memory_space=pltpu.HBM)
@@ -605,12 +641,11 @@
     return pl.pallas_call(
         body,
         out_shape=jax.ShapeDtypeStruct((ch, n, n), jnp.bfloat16),
-        in_specs=[hbm] * (5 + len(made)),
+        in_specs=[hbm] * (4 + len(made)),
         out_specs=hbm,
-        input_output_aliases={5: 0} if made else {},
+        input_output_aliases={4: 0} if made else {},
         scratch_shapes=[
-            pltpu.VMEM(weights.shape[1:], weights.dtype),
-            pltpu.VMEM((1, ch), jnp.float32),
+            pltpu.VMEM((2,) + weights.shape[1:], weights.dtype),
             pltpu.VMEM((16 * (count + 1), ch3, n), act.dtype),
             pltpu.VMEM((16 * (count + 1), ch + 8, n), held.dtype),
             pltpu.VMEM((count, ch, 16, n), jnp.bfloat16),
@@ -625,10 +660,10 @@
             flops=288 * count * ch * ch * n, bytes_accessed=200 * count * ch * n, transcendentals=0
         ),
         name="outputs",
-    )(weights, bias.reshape(1, ch), dil.reshape(1, 1), act, held, *made)
-
-
-def tile_call(gathered, weights, cot):
+    )(weights, dil.reshape(1, 1), act, held, *made)
+
+
+def tile_call(here, gathered, weights, cot):
     blocks, _, n = gathered.shape
     ch = cot.shape[0]
     assert blocks % 2 == 0
@@ -639,15 +674,16 @@
     near = 2 * MAXDIL
     units = n + 2 * near + SLOT
     return pl.pallas_call(
-        tile_kernel,
+        functools.partial(tile_kernel, here),
         out_shape=(
             jax.ShapeDtypeStruct((blocks * ch, n), f32),
             jax.ShapeDtypeStruct((blocks * ch + 3 * ch, n), f32),
             jax.ShapeDtypeStruct((n + SLOT, 3 * ch, n), bf16),
             jax.ShapeDtypeStruct((n + SLOT, ch + 8, n), f32),
+            jax.ShapeDtypeStruct((ch, n, n), bf16),
         ),
         in_specs=[vmem, hbm, hbm],
-        out_specs=(vmem, vmem, hbm, hbm),
+        out_specs=(vmem, vmem, hbm, hbm, hbm),
         scratch_shapes=[
             pltpu.VMEM((n + SLOT, 3 * ch, n), bf16),
             pltpu.VMEM((n + SLOT, ch + 8, n), f32),
@@ -666,8 +702,10 @@
             pltpu.VMEM((near, sub + 1, 8, n), f32),
             pltpu.VMEM((n, ch + 8, n), f32),
             pltpu.VMEM((ch, n, n), bf16),
-            pltpu.VMEM((4, ch, 9 * ch), bf16),
+            pltpu.VMEM((5, ch, 9 * ch), bf16),
+            pltpu.VMEM((here, ch, 16, n), bf16),
             pltpu.SemaphoreType.DMA((5,)),
+            pltpu.SemaphoreType.DMA((here,)),
         ],
         compiler_params=pltpu.CompilerParams(vmem_limit_bytes=VMEM_LIMIT),
         cost_estimate=pl.CostEstimate(
@@ -727,20 +765,20 @@
     assert cotangent.shape[2] == n == 128
     assert row_devices & (row_devices - 1) == 0 and diag_devices & (diag_devices - 1) == 0
     total_diags = n * diag_devices
-    bins, weights = pack_call(emb_cols, emb_rows, valid, dilation, band, kernel)
+    bins, weights = pack_call(emb_cols, emb_rows, valid, dilation, band, kernel, bias)
     gathered = lax.all_gather(bins, "row")
-    kept, sent, *held = tile_call(gathered, weights, cotangent)
     groups = n // 16
-    cut = groups - groups * 3 // 8
-    made = ()
+    here = groups * 5 // 8
+    kept, sent, *held, pair_out = tile_call(here, gathered, weights, cotangent)
+    made = None
 
     place = lax.axis_index("row")
     bit = row_devices // 2
     while True:
         came = swapped(sent, "row", bit)
-        if not made:
-            made = (out_call(0, cut, (), weights, bias, dilation, *held),)
-            came, *made = lax.optimization_barrier((came, *made))
+        if made is None:
+            made = out_call(here, groups - here, (pair_out,), weights, dilation, *held)
+            came, made = lax.optimization_barrier((came, made))
         own = bit * 2 * ch
         sums, whole = kept + came[:own], sent[own:] + came[own:]
         bit //= 2
@@ -757,15 +795,13 @@
         both = both + swapped(both, "diag", bit)
         bit *= 2
     came = swapped(both, "diag", bit)
-    pair_out = out_call(cut, groups - cut, tuple(made), weights, bias, dilation, *held)
-    came, pair_out = lax.optimization_barrier((came, pair_out))
     rows, cols, kgrad, bgrad = final_call(
         both,
         came,
         1.0 / total_diags**0.5,
         1.0 / (row_devices * n * total_diags) ** 0.5,
     )
-    return pair_out, rows, cols, kgrad.reshape(3, 3, ch, ch), bgrad.reshape(ch)
+    return made, rows, cols, kgrad.reshape(3, 3, ch, ch), bgrad.reshape(ch)
 
 
 def solution(mesh):

time: 43 us -> 42.1 us (0.979)
  Pallas kernels: 23.5 us -> 19.8 us
  waiting for transfers between devices: 4.14 us -> 7.01 us
    pallas_call x2 -> x1, Pallas kernels: 8.71 us -> 3.74 us  [out_call(): pl.pallas_call(body, out_shape=jax.ShapeDtypeStruct((ch, n, n), jnp.bfloa...]
    ppermute x4, waiting for transfers between devices: 4.14 us -> 7.01 us  [swapped(): lax.ppermute(value, axis, [(i, i ^ bit) for i in range(lax.axis_size(axis...]
    pallas_call x1, Pallas kernels: 12.2 us -> 13.4 us  [tile_call(): pl.pallas_call(functools.partial(tile_kernel, here), out_shape=(jax.Shape...]
  transfers between devices with their start and end apart: 4 -> 4, of which waited for: 2 -> 3; matrix products, arithmetic and copies ran while one was open for 0% -> 0% of each run, Pallas kernels for 20% -> 9%
where the time goes in v4:
time: 42.1 us; the launch traced here: 42 us
  Pallas kernels  19.8 us (47%)
  waiting for transfers between devices  7.01 us (17%)
  starting transfers between devices  6.67 us (16%)
  blocking collectives  6.51 us (15%)
  between operations  2 us (5%)
    pallas_call x1, Pallas kernels, tile_call(): pl.pallas_call(functools.partial(tile_kernel, here), out_shape=(jax.Shape...  13.4 us
    ppermute x4, waiting for transfers between devices, swapped(): lax.ppermute(value, axis, [(i, i ^ bit) for i in range(lax.axis_size(axis...  7.01 us
    ppermute x4, starting transfers between devices, swapped(): lax.ppermute(value, axis, [(i, i ^ bit) for i in range(lax.axis_size(axis...  6.67 us
    all_gather x1, blocking collectives, local(): gathered = lax.all_gather(bins, 'row')  6.51 us
    pallas_call x1, Pallas kernels, out_call(): pl.pallas_call(body, out_shape=jax.ShapeDtypeStruct((ch, n, n), jnp.bfloa...  3.74 us
    pallas_call x1, Pallas kernels, pack_call(): pl.pallas_call(pack_kernel, out_shape=(jax.ShapeDtypeStruct((2 * ch + 16,...  1.86 us
  transfers between devices with their start and end apart: 4, of which 3 were waited for; matrix products, arithmetic and copies ran while one was open for 0% of the time, Pallas kernels for 9%

profile of v4, /device:TPU:0, one launch (start us, length us, event | category | flops | bytes accessed | tf_op | source)
XLA Modules:
  0.0 42.0 jit_solution(661540308994527424)
XLA Ops:
  1.9 1.9 %pack.1 = (bf16[80,128]{1,0:T(8,128)(2,1)}, bf16[16,32,288]{2,1,0:T(8,128)(2,1)}) custom-call(bf16[32,128]{1,0:T(8,128)(2,1)} %emb_cols.1, bf16[32,128]{1,0:T(8,128)(2,1)} %emb_rows.1, s32[1,128]{1,0:T(1,128)} %bitcast.18, s32[1,1]{1,0:T(1,128)} %bitcast.12.dil, s32[1,1]{1,0:T(1,128)} %bitcast.14.band, bf16[3,3,32,32]{3,2,1,0:T(8,128)(2,1)} %kernel.1, ...), custom_call_target="tpu_custom_call" | custom-call | tf_op jit(solution)/shard_map/pack/pallas_call | solution.py:69
  3.8 6.5 %all-gather = bf16[320,128]{1,0:T(8,128)(2,1)S(1)} all-gather(bf16[80,128]{1,0:T(8,128)(2,1)} %get-tuple-element.18), channel_id=2, replica_groups=mesh['grp'=2,'row'=4,'diag'=4] {'row'}, dimensions={0}, use_global_device_ids=true | all-gather | bytes 102400 | tf_op jit(solution)/shard_map/all_gather | solution.py:769
  10.3 13.4 %tile.1 = (f32[128,128]{1,0:T(8,128)S(1)}, f32[224,128]{1,0:T(8,128)S(1)}, bf16[144,96,128]{2,1,0:T(8,128)(2,1)}, f32[144,40,128]{2,1,0:T(8,128)}, bf16[32,128,128]{2,1,0:T(8,128)(2,1)}) custom-call(bf16[4,80,128]{2,1,0:T(8,128)(2,1)S(1)} %bitcast.15, bf16[16,32,288]{2,1,0:T(8,128)(2,1)} %get-tuple-element.19.weights_hbm.refs_0_, bf16[32,128,128]{2,1,0:T(8,128)(2,1)} %cot_hbm.1), custom_call_target="tpu_custom_call" | custom-call | flops 905969664 | bytes 8388608 | tf_op jit(solution)/shard_map/tile/pallas_call | solution.py:676
  23.7 2.0 %collective-permute-start = (f32[224,128]{1,0:T(8,128)S(1)}, f32[224,128]{1,0:T(8,128)S(1)}, u32[]{:S(2)}, u32[]{:S(2)}) collective-permute-start(f32[224,128]{1,0:T(8,128)S(1)} %get-tuple-element.20), channel_id=1, source_target_pairs={{0,8},{4,12},{8,0},{12,4},{1,9},{5,13},{9,1},{13,5},{2,10},{6,14},... | collective-permute-start | bytes 344072 | tf_op jit(solution)/shard_map/ppermute | solution.py:759
  25.7 3.7 %outputs.1 = bf16[32,128,128]{2,1,0:T(8,128)(2,1)} custom-call(bf16[16,32,288]{2,1,0:T(8,128)(2,1)} %get-tuple-element.19.weights_hbm.refs_0_, s32[1,1]{1,0:T(1,128)} %bitcast.13.refs_1_, bf16[144,96,128]{2,1,0:T(8,128)(2,1)} %get-tuple-element.21.refs_2_, f32[144,40,128]{2,1,0:T(8,128)} %get-tuple-element.22.refs_3_, ...), custom_call_target="tpu_custom_call", output_to_operand_aliasing={{}: (4, {})} | custom-call | flops 113246208 | bytes 2457600 | tf_op jit(solution)/shard_map/outputs/pallas_call | solution.py:641
  29.5 0.0 collective-permute-done
  29.6 0.1 collective-permute-start.1
  29.7 1.2 %collective-permute-done.1 = f32[160,128]{1,0:T(8,128)S(1)} collective-permute-done((f32[160,128]{1,0:T(8,128)S(1)}, f32[160,128]{1,0:T(8,128)S(1)}, u32[]{:S(2)}, u32[]{:S(2)}) %collective-permute-start.1) | collective-permute-done | bytes 81952 | tf_op jit(solution)/shard_map/ppermute | solution.py:759
  31.0 1.7 %collective-permute-start.2 = (f32[160,128]{1,0:T(8,128)S(1)}, f32[160,128]{1,0:T(8,128)S(1)}, u32[]{:S(2)}, u32[]{:S(2)}) collective-permute-start(f32[160,128]{1,0:T(8,128)S(1)} %pad_maximum_fusion.1), channel_id=1, source_target_pairs={{0,1},{1,0},{2,3},{3,2},{4,5},{5,4},{6,7},{7,6},{8,9},{9,8},{10,11... | collective-permute-start | bytes 245768 | tf_op jit(solution)/shard_map/ppermute | solution.py:759
  32.7 2.8 %collective-permute-done.2 = f32[160,128]{1,0:T(8,128)S(1)} collective-permute-done((f32[160,128]{1,0:T(8,128)S(1)}, f32[160,128]{1,0:T(8,128)S(1)}, u32[]{:S(2)}, u32[]{:S(2)}) %collective-permute-start.2) | collective-permute-done | bytes 81952 | tf_op jit(solution)/shard_map/ppermute | solution.py:759
  35.5 2.8 %collective-permute-start.3 = (f32[160,128]{1,0:T(8,128)S(1)}, f32[160,128]{1,0:T(8,128)S(1)}, u32[]{:S(2)}, u32[]{:S(2)}) collective-permute-start(f32[160,128]{1,0:T(8,128)S(1)} %fusion.refs_0_), channel_id=1, source_target_pairs={{0,2},{1,3},{2,0},{3,1},{4,6},{5,7},{6,4},{7,5},{8,10},{9,11},{10,... | collective-permute-start | bytes 245768 | tf_op jit(solution)/shard_map/ppermute | solution.py:759
  38.3 3.0 %collective-permute-done.3.refs_1_ = f32[160,128]{1,0:T(8,128)S(1)} collective-permute-done((f32[160,128]{1,0:T(8,128)S(1)}, f32[160,128]{1,0:T(8,128)S(1)}, u32[]{:S(2)}, u32[]{:S(2)}) %collective-permute-start.3) | collective-permute-done | bytes 81952 | tf_op jit(solution)/shard_map/ppermute | solution.py:759
  41.3 0.8 %finish.1 = (f32[32,128]{1,0:T(8,128)}, f32[32,128]{1,0:T(8,128)}, f32[9,32,32]{2,1,0:T(8,128)}, f32[1,32]{1,0:T(1,128)}) custom-call(f32[160,128]{1,0:T(8,128)S(1)} %fusion.refs_0_, f32[160,128]{1,0:T(8,128)S(1)} %collective-permute-done.3.refs_1_), custom_call_target="tpu_custom_call" | custom-call | tf_op jit(solution)/shard_map/finish/pallas_call | solution.py:743
  (8 shorter events, 0.1 us)
Async XLA Ops:
  23.7 5.8 %collective-permute-start = (f32[224,128]{1,0:T(8,128)S(1)}, f32[224,128]{1,0:T(8,128)S(1)}, u32[]{:S(2)}, u32[]{:S(2)}) collective-permute-start(f32[224,128]{1,0:T(8,128)S(1)} %get-tuple-element.20), channel_id=1, source_target_pairs={{0,8},{4,12},{8,0},{12,4},{1,9},{5,13},{9,1},{13,5},{2,10},{6,14},... | collective-permute-start | bytes 344072 | tf_op jit(solution)/shard_map/ppermute | solution.py:759
  29.6 1.3 %collective-permute-start.1 = (f32[160,128]{1,0:T(8,128)S(1)}, f32[160,128]{1,0:T(8,128)S(1)}, u32[]{:S(2)}, u32[]{:S(2)}) collective-permute-start(f32[160,128]{1,0:T(8,128)S(1)} %pad_maximum_fusion), channel_id=1, source_target_pairs={{0,4},{4,0},{8,12},{12,8},{1,5},{5,1},{9,13},{13,9},{2,6},{6,2},{1... | collective-permute-start | bytes 245768 | tf_op jit(solution)/shard_map/ppermute | solution.py:759
  31.0 4.6 %collective-permute-start.2 = (f32[160,128]{1,0:T(8,128)S(1)}, f32[160,128]{1,0:T(8,128)S(1)}, u32[]{:S(2)}, u32[]{:S(2)}) collective-permute-start(f32[160,128]{1,0:T(8,128)S(1)} %pad_maximum_fusion.1), channel_id=1, source_target_pairs={{0,1},{1,0},{2,3},{3,2},{4,5},{5,4},{6,7},{7,6},{8,9},{9,8},{10,11... | collective-permute-start | bytes 245768 | tf_op jit(solution)/shard_map/ppermute | solution.py:759
  35.5 5.7 %collective-permute-start.3 = (f32[160,128]{1,0:T(8,128)S(1)}, f32[160,128]{1,0:T(8,128)S(1)}, u32[]{:S(2)}, u32[]{:S(2)}) collective-permute-start(f32[160,128]{1,0:T(8,128)S(1)} %fusion.refs_0_), channel_id=1, source_target_pairs={{0,2},{1,3},{2,0},{3,1},{4,6},{5,7},{6,4},{7,5},{8,10},{9,11},{10,... | collective-permute-start | bytes 245768 | tf_op jit(solution)/shard_map/ppermute | solution.py:759

commit v5 on v4

--- a/solution.py
+++ b/solution.py
@@ -462,11 +462,8 @@
             accs[which] += jnp.where((lane8 == (i & (n - 1)))[None], total, 0.0)
         return kernel_part(i0)
 
-    def near_pair(g, carry):
-        kacc[...] += near_sums(4 * g) + near_sums(4 * g + 2)
-        return carry
-
-    lax.fori_loop(0, extra // 2, near_pair, 0)
+    parts = [near_sums(y) for y in range(0, 2 * extra, 2)]
+    kacc[...] += (parts[0] + parts[1]) + (parts[2] + parts[3])
 
     def pack_sums(g, carry):
         for two in range(4):

time: 42.1 us -> 41.9 us (level)
  Pallas kernels: 19.8 us -> 19.3 us
    pallas_call x1, Pallas kernels: 13.4 us -> 12.9 us  [tile_call(): pl.pallas_call(functools.partial(tile_kernel, here), out_shape=(jax.Shape...]
where the time goes in v5:
time: 41.9 us; the launch traced here: 41.5 us
  Pallas kernels  19.3 us (46%)
  waiting for transfers between devices  7 us (17%)
  starting transfers between devices  6.69 us (16%)
  blocking collectives  6.51 us (16%)
  between operations  2 us (5%)
    pallas_call x1, Pallas kernels, tile_call(): pl.pallas_call(functools.partial(tile_kernel, here), out_shape=(jax.Shape...  12.9 us
    ppermute x4, waiting for transfers between devices, swapped(): lax.ppermute(value, axis, [(i, i ^ bit) for i in range(lax.axis_size(axis...  7 us
    ppermute x4, starting transfers between devices, swapped(): lax.ppermute(value, axis, [(i, i ^ bit) for i in range(lax.axis_size(axis...  6.69 us
    all_gather x1, blocking collectives, local(): gathered = lax.all_gather(bins, 'row')  6.51 us
    pallas_call x1, Pallas kernels, out_call(): pl.pallas_call(body, out_shape=jax.ShapeDtypeStruct((ch, n, n), jnp.bfloa...  3.73 us
    pallas_call x1, Pallas kernels, pack_call(): pl.pallas_call(pack_kernel, out_shape=(jax.ShapeDtypeStruct((2 * ch + 16,...  1.86 us
  transfers between devices with their start and end apart: 4, of which 3 were waited for; matrix products, arithmetic and copies ran while one was open for 0% of the time, Pallas kernels for 9%

profile of v5, /device:TPU:0, one launch (start us, length us, event | category | flops | bytes accessed | tf_op | source)
XLA Modules:
  0.0 41.5 jit_solution(12529915874551553230)
XLA Ops:
  1.9 1.9 %pack.1 = (bf16[80,128]{1,0:T(8,128)(2,1)}, bf16[16,32,288]{2,1,0:T(8,128)(2,1)}) custom-call(bf16[32,128]{1,0:T(8,128)(2,1)} %emb_cols.1, bf16[32,128]{1,0:T(8,128)(2,1)} %emb_rows.1, s32[1,128]{1,0:T(1,128)} %bitcast.18, s32[1,1]{1,0:T(1,128)} %bitcast.12.dil, s32[1,1]{1,0:T(1,128)} %bitcast.14.band, bf16[3,3,32,32]{3,2,1,0:T(8,128)(2,1)} %kernel.1, ...), custom_call_target="tpu_custom_call" | custom-call | tf_op jit(solution)/shard_map/pack/pallas_call | solution.py:69
  3.8 6.5 %all-gather = bf16[320,128]{1,0:T(8,128)(2,1)S(1)} all-gather(bf16[80,128]{1,0:T(8,128)(2,1)} %get-tuple-element.18), channel_id=2, replica_groups=mesh['grp'=2,'row'=4,'diag'=4] {'row'}, dimensions={0}, use_global_device_ids=true | all-gather | bytes 102400 | tf_op jit(solution)/shard_map/all_gather | solution.py:766
  10.3 12.9 %tile.1 = (f32[128,128]{1,0:T(8,128)S(1)}, f32[224,128]{1,0:T(8,128)S(1)}, bf16[144,96,128]{2,1,0:T(8,128)(2,1)}, f32[144,40,128]{2,1,0:T(8,128)}, bf16[32,128,128]{2,1,0:T(8,128)(2,1)}) custom-call(bf16[4,80,128]{2,1,0:T(8,128)(2,1)S(1)} %bitcast.15, bf16[16,32,288]{2,1,0:T(8,128)(2,1)} %get-tuple-element.19.weights_hbm.refs_0_, bf16[32,128,128]{2,1,0:T(8,128)(2,1)} %cot_hbm.1), custom_call_target="tpu_custom_call" | custom-call | flops 905969664 | bytes 8388608 | tf_op jit(solution)/shard_map/tile/pallas_call | solution.py:673
  23.2 2.0 %collective-permute-start = (f32[224,128]{1,0:T(8,128)S(1)}, f32[224,128]{1,0:T(8,128)S(1)}, u32[]{:S(2)}, u32[]{:S(2)}) collective-permute-start(f32[224,128]{1,0:T(8,128)S(1)} %get-tuple-element.20), channel_id=1, source_target_pairs={{0,8},{4,12},{8,0},{12,4},{1,9},{5,13},{9,1},{13,5},{2,10},{6,14},... | collective-permute-start | bytes 344072 | tf_op jit(solution)/shard_map/ppermute | solution.py:756
  25.3 3.7 %outputs.1 = bf16[32,128,128]{2,1,0:T(8,128)(2,1)} custom-call(bf16[16,32,288]{2,1,0:T(8,128)(2,1)} %get-tuple-element.19.weights_hbm.refs_0_, s32[1,1]{1,0:T(1,128)} %bitcast.13.refs_1_, bf16[144,96,128]{2,1,0:T(8,128)(2,1)} %get-tuple-element.21.refs_2_, f32[144,40,128]{2,1,0:T(8,128)} %get-tuple-element.22.refs_3_, ...), custom_call_target="tpu_custom_call", output_to_operand_aliasing={{}: (4, {})} | custom-call | flops 113246208 | bytes 2457600 | tf_op jit(solution)/shard_map/outputs/pallas_call | solution.py:638
  29.0 0.0 collective-permute-done
  29.1 0.1 collective-permute-start.1
  29.2 1.2 %collective-permute-done.1 = f32[160,128]{1,0:T(8,128)S(1)} collective-permute-done((f32[160,128]{1,0:T(8,128)S(1)}, f32[160,128]{1,0:T(8,128)S(1)}, u32[]{:S(2)}, u32[]{:S(2)}) %collective-permute-start.1) | collective-permute-done | bytes 81952 | tf_op jit(solution)/shard_map/ppermute | solution.py:756
  30.5 1.8 %collective-permute-start.2 = (f32[160,128]{1,0:T(8,128)S(1)}, f32[160,128]{1,0:T(8,128)S(1)}, u32[]{:S(2)}, u32[]{:S(2)}) collective-permute-start(f32[160,128]{1,0:T(8,128)S(1)} %pad_maximum_fusion.1), channel_id=1, source_target_pairs={{0,1},{1,0},{2,3},{3,2},{4,5},{5,4},{6,7},{7,6},{8,9},{9,8},{10,11... | collective-permute-start | bytes 245768 | tf_op jit(solution)/shard_map/ppermute | solution.py:756
  32.2 2.8 %collective-permute-done.2 = f32[160,128]{1,0:T(8,128)S(1)} collective-permute-done((f32[160,128]{1,0:T(8,128)S(1)}, f32[160,128]{1,0:T(8,128)S(1)}, u32[]{:S(2)}, u32[]{:S(2)}) %collective-permute-start.2) | collective-permute-done | bytes 81952 | tf_op jit(solution)/shard_map/ppermute | solution.py:756
  35.0 2.8 %collective-permute-start.3 = (f32[160,128]{1,0:T(8,128)S(1)}, f32[160,128]{1,0:T(8,128)S(1)}, u32[]{:S(2)}, u32[]{:S(2)}) collective-permute-start(f32[160,128]{1,0:T(8,128)S(1)} %fusion.refs_0_), channel_id=1, source_target_pairs={{0,2},{1,3},{2,0},{3,1},{4,6},{5,7},{6,4},{7,5},{8,10},{9,11},{10,... | collective-permute-start | bytes 245768 | tf_op jit(solution)/shard_map/ppermute | solution.py:756
  37.8 3.0 %collective-permute-done.3.refs_1_ = f32[160,128]{1,0:T(8,128)S(1)} collective-permute-done((f32[160,128]{1,0:T(8,128)S(1)}, f32[160,128]{1,0:T(8,128)S(1)}, u32[]{:S(2)}, u32[]{:S(2)}) %collective-permute-start.3) | collective-permute-done | bytes 81952 | tf_op jit(solution)/shard_map/ppermute | solution.py:756
  40.8 0.8 %finish.1 = (f32[32,128]{1,0:T(8,128)}, f32[32,128]{1,0:T(8,128)}, f32[9,32,32]{2,1,0:T(8,128)}, f32[1,32]{1,0:T(1,128)}) custom-call(f32[160,128]{1,0:T(8,128)S(1)} %fusion.refs_0_, f32[160,128]{1,0:T(8,128)S(1)} %collective-permute-done.3.refs_1_), custom_call_target="tpu_custom_call" | custom-call | tf_op jit(solution)/shard_map/finish/pallas_call | solution.py:740
  (8 shorter events, 0.1 us)
Async XLA Ops:
  23.2 5.8 %collective-permute-start = (f32[224,128]{1,0:T(8,128)S(1)}, f32[224,128]{1,0:T(8,128)S(1)}, u32[]{:S(2)}, u32[]{:S(2)}) collective-permute-start(f32[224,128]{1,0:T(8,128)S(1)} %get-tuple-element.20), channel_id=1, source_target_pairs={{0,8},{4,12},{8,0},{12,4},{1,9},{5,13},{9,1},{13,5},{2,10},{6,14},... | collective-permute-start | bytes 344072 | tf_op jit(solution)/shard_map/ppermute | solution.py:756
  29.1 1.3 %collective-permute-start.1 = (f32[160,128]{1,0:T(8,128)S(1)}, f32[160,128]{1,0:T(8,128)S(1)}, u32[]{:S(2)}, u32[]{:S(2)}) collective-permute-start(f32[160,128]{1,0:T(8,128)S(1)} %pad_maximum_fusion), channel_id=1, source_target_pairs={{0,4},{4,0},{8,12},{12,8},{1,5},{5,1},{9,13},{13,9},{2,6},{6,2},{1... | collective-permute-start | bytes 245768 | tf_op jit(solution)/shard_map/ppermute | solution.py:756
  30.5 4.6 %collective-permute-start.2 = (f32[160,128]{1,0:T(8,128)S(1)}, f32[160,128]{1,0:T(8,128)S(1)}, u32[]{:S(2)}, u32[]{:S(2)}) collective-permute-start(f32[160,128]{1,0:T(8,128)S(1)} %pad_maximum_fusion.1), channel_id=1, source_target_pairs={{0,1},{1,0},{2,3},{3,2},{4,5},{5,4},{6,7},{7,6},{8,9},{9,8},{10,11... | collective-permute-start | bytes 245768 | tf_op jit(solution)/shard_map/ppermute | solution.py:756
  35.0 5.7 %collective-permute-start.3 = (f32[160,128]{1,0:T(8,128)S(1)}, f32[160,128]{1,0:T(8,128)S(1)}, u32[]{:S(2)}, u32[]{:S(2)}) collective-permute-start(f32[160,128]{1,0:T(8,128)S(1)} %fusion.refs_0_), channel_id=1, source_target_pairs={{0,2},{1,3},{2,0},{3,1},{4,6},{5,7},{6,4},{7,5},{8,10},{9,11},{10,... | collective-permute-start | bytes 245768 | tf_op jit(solution)/shard_map/ppermute | solution.py:756
